TPU v7x, 128 devices: a whole 4x4x4 slice. The times are simulated.
128 devices in a mesh: row: 16 (over x_hi, z, core), col: 8 (over x_lo, y).
Axes of the slice: x: 4 (x_hi: 2, x_lo: 2; x = x_hi * 2 + x_lo), y: 4, z: 4, core: 2. Of those that a mesh axis runs over, the one named last changes fastest.
Arguments:
- tokens: bfloat16 [65536, 6144], P(('row', 'col')), may hold values from -6 to 6
- grad_out: bfloat16 [65536, 6144], P(('row', 'col')), may hold values from -6 to 6
- w_up: bfloat16 [6144, 512], replicated, may hold values from -0.078125 to 0.078125
- w_down: bfloat16 [512, 6144], replicated, may hold values from -0.0390625 to 0.0390625
Outputs:
- up_grad: float32 [6144, 512], P('row', 'col')
- down_grad: float32 [6144, 512], P('row', 'col')
All inputs are finite; a program needn't handle non-finite values.
Results may differ from a plain program's by a relative error of at most 0.0041.
Values may be sent and summed in bfloat16 or wider, within the bound.
No kernel may reach another device: no remote copies, remote signals or barrier semaphores. Data moves between devices by JAX's collectives and lax.ppermute only.
A program may use at most 128 MiB of HBM per device.

v0:
```python
import math

import jax
import jax.numpy as jnp
from jax import lax
from jax.sharding import PartitionSpec as P


def gelu_parts(preact):
    cumul = 0.5 * (1.0 + jax.scipy.special.erf(preact / math.sqrt(2.0)))
    density = jnp.exp(-0.5 * preact * preact) / math.sqrt(2.0 * math.pi)
    return (preact * cumul, cumul + preact * density)


def reduce_bucket(term):
    levels = term.astype(jnp.bfloat16)
    rows, cols = levels.shape
    row_count = lax.axis_size("row")
    col_count = lax.axis_size("col")
    piece_rows = rows // row_count
    piece_cols = cols // col_count
    owners = row_count * col_count
    level_blocks = (
        levels.reshape(row_count, piece_rows, col_count, piece_cols)
        .transpose(0, 2, 1, 3)
        .reshape(owners, piece_rows, piece_cols)
    )
    got_levels = lax.all_to_all(
        level_blocks, ("row", "col"), split_axis=0, concat_axis=0, tiled=True
    )
    return jnp.sum(got_levels, axis=0, dtype=jnp.float32)


def local(tokens, grad_out, w_up, w_down):
    preact = jnp.dot(tokens, w_up, preferred_element_type=jnp.float32)
    act_grad = lax.dot_general(
        grad_out, w_down, (((1,), (1,)), ((), ())), preferred_element_type=jnp.float32
    )
    value, slope = gelu_parts(preact)
    act = value.astype(jnp.bfloat16)
    hidden_grad = (act_grad * slope).astype(jnp.bfloat16)
    term_up = lax.dot_general(
        tokens, hidden_grad, (((0,), (0,)), ((), ())), preferred_element_type=jnp.float32
    )
    summed_up = reduce_bucket(term_up)
    term_down = lax.dot_general(
        grad_out, act, (((0,), (0,)), ((), ())), preferred_element_type=jnp.float32
    )
    summed_down = reduce_bucket(term_down)
    total_tokens = tokens.shape[0] * lax.axis_size("row") * lax.axis_size("col")
    factor = 1.0 / math.sqrt(total_tokens)
    return (summed_up * factor, summed_down * factor)


def solution(mesh):
    placed = (P(("row", "col"), None), P(("row", "col"), None), P(), P())
    return jax.shard_map(
        local,
        mesh=mesh,
        in_specs=placed,
        out_specs=(P("row", "col"), P("row", "col")),
        check_vma=False,
    )
```

profile of v0, /device:TPU:17, one launch (start us, length us, event | category | flops | bytes accessed | tf_op | source)
XLA Modules:
  0.0 201.3 jit_solution(16235122465278878615)
XLA Ops:
  0.6 0.0 copy-start
  0.6 7.6 %fusion.9 = f32[512,512]{1,0:T(8,128)S(1)} fusion(bf16[512,6144]{1,0:T(8,128)(2,1)} %param.4, bf16[6144,512]{1,0:T(8,128)(2,1)} %param.6), kind=kOutput, calls=%fused_computation.19 | convolution fusion | flops 3221225472 | bytes 13631488 | tf_op jit(solution)/shard_map/dot_general | solution.py:35
  8.2 0.0 copy-done
  8.3 3.9 %convolution_convert_fusion = bf16[512,6144]{1,0:T(8,128)(2,1)S(1)} fusion(bf16[512,6144]{1,0:T(8,128)(2,1)S(1)} %copy-done, f32[512,512]{1,0:T(8,128)S(1)} %fusion.9), kind=kOutput, calls=%fused_computation.2 | convolution fusion | flops 3225681920 | bytes 13631488 | tf_op jit(solution)/shard_map/dot_general | solution.py:46
  12.2 1.6 copy.9
  13.8 4.2 %copy.7 = bf16[16,384,8,64]{1,3,2,0:T(8,128)(2,1)} copy(bf16[16,384,8,64]{1,0,3,2:T(8,128)(2,1)S(1)} %bitcast.26) | data formatting | bytes 12582912 | tf_op jit(solution)/shard_map/reshape | solution.py:24
  18.1 11.0 %all-to-all-start.1 = ((bf16[128,384,64]{1,2,0:T(8,128)(2,1)}), bf16[128,384,64]{1,2,0:T(8,128)(2,1)}, u32[]{:S(2)}, u32[]{:S(2)}) async-start(bf16[128,384,64]{1,2,0:T(8,128)(2,1)} %bitcast.25), calls=%async_computation.1 | async-start | bytes 12582912 | tf_op jit(solution)/shard_map/all_to_all | solution.py:28
  29.1 16.0 %convolution_convert_fusion.1 = bf16[512,6144]{1,0:T(8,128)(2,1)} fusion(bf16[512,6144]{1,0:T(8,128)(2,1)} %param.4, bf16[512,6144]{1,0:T(8,128)(2,1)} %param.5, bf16[512,6144]{1,0:T(8,128)(2,1)} %param.7, f32[512,512]{1,0:T(8,128)S(1)} %fusion.9), kind=kOutput, calls=%fused_computation.3 | convolution fusion | flops 6448218112 | bytes 26214400 | tf_op jit(solution)/shard_map/dot_general | solution.py:42
  45.1 4.4 %copy.8 = bf16[64,8,16,384]{3,2,1,0:T(8,128)(2,1)S(1)} copy(bf16[64,8,16,384]{3,1,2,0:T(8,128)(2,1)} %bitcast.29) | data formatting | bytes 12582912
  49.5 4.2 %copy.6 = bf16[16,384,8,64]{1,3,2,0:T(8,128)(2,1)} copy(bf16[16,384,8,64]{1,0,3,2:T(8,128)(2,1)S(1)} %bitcast.27) | data formatting | bytes 12582912 | tf_op jit(solution)/shard_map/reshape | solution.py:24
  53.7 56.3 %all-to-all-done.1 = bf16[128,384,64]{1,2,0:T(8,128)(2,1)} async-done(((bf16[128,384,64]{1,2,0:T(8,128)(2,1)}), bf16[128,384,64]{1,2,0:T(8,128)(2,1)}, u32[]{:S(2)}, u32[]{:S(2)}) %all-to-all-start.1) | async-done | bytes 6291488 | tf_op jit(solution)/shard_map/all_to_all | solution.py:28
  110.0 6.0 %all-to-all-start = ((bf16[128,384,64]{1,2,0:T(8,128)(2,1)}), bf16[128,384,64]{1,2,0:T(8,128)(2,1)}, u32[]{:S(2)}, u32[]{:S(2)}) async-start(bf16[128,384,64]{1,2,0:T(8,128)(2,1)} %bitcast.24), calls=%async_computation | async-start | bytes 12582912 | tf_op jit(solution)/shard_map/all_to_all | solution.py:28
  116.1 3.7 %convert_reduce_fusion = f32[384,64]{0,1:T(8,128)S(1)} fusion(bf16[128,384,64]{1,2,0:T(8,128)(2,1)} %all-to-all-done.1), kind=kLoop, calls=%fused_computation | loop fusion | flops 6266880 | bytes 6389760 | tf_op jit(solution)/shard_map/reduce_sum | solution.py:31
  119.8 0.6 broadcast_multiply_fusion
  120.4 76.5 %all-to-all-done = bf16[128,384,64]{1,2,0:T(8,128)(2,1)} async-done(((bf16[128,384,64]{1,2,0:T(8,128)(2,1)}), bf16[128,384,64]{1,2,0:T(8,128)(2,1)}, u32[]{:S(2)}, u32[]{:S(2)}) %all-to-all-start) | async-done | bytes 6291488 | tf_op jit(solution)/shard_map/all_to_all | solution.py:28
  196.9 3.7 %convert_reduce_fusion.1 = f32[384,64]{0,1:T(8,128)S(1)} fusion(bf16[128,384,64]{1,2,0:T(8,128)(2,1)} %all-to-all-done), kind=kLoop, calls=%fused_computation.1 | loop fusion | flops 6266880 | bytes 6389760 | tf_op jit(solution)/shard_map/reduce_sum | solution.py:31
  200.6 0.6 broadcast_multiply_fusion.1
Async XLA Ops:
  0.6 7.6 %copy-start = (bf16[512,6144]{1,0:T(8,128)(2,1)S(1)}, bf16[512,6144]{1,0:T(8,128)(2,1)}, u32[]{:S(2)}) copy-start(bf16[512,6144]{1,0:T(8,128)(2,1)} %param.5) | copy-start | bytes 18874372
  18.1 91.9 %all-to-all-start.1 = ((bf16[128,384,64]{1,2,0:T(8,128)(2,1)}), bf16[128,384,64]{1,2,0:T(8,128)(2,1)}, u32[]{:S(2)}, u32[]{:S(2)}) async-start(bf16[128,384,64]{1,2,0:T(8,128)(2,1)} %bitcast.25), calls=%async_computation.1 | async-start | bytes 12582912 | tf_op jit(solution)/shard_map/all_to_all | solution.py:28
  110.0 86.9 %all-to-all-start = ((bf16[128,384,64]{1,2,0:T(8,128)(2,1)}), bf16[128,384,64]{1,2,0:T(8,128)(2,1)}, u32[]{:S(2)}, u32[]{:S(2)}) async-start(bf16[128,384,64]{1,2,0:T(8,128)(2,1)} %bitcast.24), calls=%async_computation | async-start | bytes 12582912 | tf_op jit(solution)/shard_map/all_to_all | solution.py:28
where the time goes:
time: 202 us; the launch traced here: 201 us
  waiting for transfers between devices  133 us (66%)
  matrix products  27.5 us (14%)
  starting transfers between devices  17.1 us (8%)
  local copies, waits for them, and re-layouts  14.5 us (7%)
  other arithmetic  8.68 us (4%)
    all_to_all x2, waiting for transfers between devices, reduce_bucket(): lax.all_to_all(level_blocks, ('row', 'col'), split_axis=0, concat_axis=0,...  133 us
    all_to_all x2, starting transfers between devices, reduce_bucket(): lax.all_to_all(level_blocks, ('row', 'col'), split_axis=0, concat_axis=0,...  17.1 us
    dot_general x1, matrix products, local(): lax.dot_general(tokens, hidden_grad, (((0,), (0,)), ((), ())), preferred_...  16 us
    reshape x2, local copies, waits for them, and re-layouts, reduce_bucket(): levels.reshape(row_count, piece_rows, col_count, piece_cols)  8.45 us
    dot_general x1, matrix products, local(): preact = jnp.dot(tokens, w_up, preferred_element_type=jnp.float32)  7.6 us
    reduce_sum x2, other arithmetic, reduce_bucket(): return jnp.sum(got_levels, axis=0, dtype=jnp.float32)  7.39 us
    unnamed x4, local copies, waits for them, and re-layouts  6.08 us
  transfers between devices with their start and end apart: 2, of which 2 were waited for; matrix products, arithmetic and copies ran while one was open for 14% of the time, Pallas kernels for 0%

commit v1 on v0

v1 whole, which is shorter than its diff:
```python
import functools
import math

import jax
import jax.numpy as jnp
from jax import lax
from jax.experimental import pallas as pl
from jax.experimental.pallas import tpu as pltpu
from jax.sharding import PartitionSpec as P


AXES = ("row", "col")
TOK = 512
HID = 512
WIDTH = 6144
LANES = 128
SUB = 64
COLORS = 3
HALF = WIDTH // 2
BF16 = jnp.bfloat16
F32 = jnp.float32


def coords(index):
    row, col = divmod(index, 8)
    xh, rest = divmod(row, 8)
    z, core = divmod(rest, 2)
    xl, y = divmod(col, 4)
    return xh * 2 + xl, y, z, core


def linear(x, y, z, core):
    x, y, z = x % 4, y % 4, z % 4
    return ((x // 2) * 8 + z * 2 + core) * 8 + (x % 2) * 4 + y


def shift(value, axis0, axis1, step):
    pairs = []
    for index in range(128):
        x, y, z, core = coords(index)
        place = {"x": x, "y": y, "z": z}
        place[axis0 if core == 0 else axis1] += step
        pairs.append((index, linear(place["x"], place["y"], place["z"], core)))
    return lax.ppermute(value, AXES, pairs)


def swap(value):
    pairs = []
    for index in range(128):
        x, y, z, core = coords(index)
        pairs.append((index, linear(x, y, z, 1 - core)))
    return lax.ppermute(value, AXES, pairs)


def limit(mib):
    return pltpu.CompilerParams(vmem_limit_bytes=mib * 1024 * 1024)


def cost(flops, bytes_accessed):
    return pl.CostEstimate(flops=flops, bytes_accessed=bytes_accessed, transcendentals=0)


VMEM = pl.BlockSpec(memory_space=pltpu.VMEM)
SMEM = pl.BlockSpec(memory_space=pltpu.SMEM)
ANY = pl.BlockSpec(memory_space=pl.ANY)
LIM = 12
CHUNK = 2 * COLORS * LANES
CHUNKS = WIDTH // CHUNK


def pack_columns(meta, step, block_ref, peer_ref):
    core, own_z = meta[0], meta[3]
    xh, z = step // 4, step % 4
    j = (z - own_z + 4) % 4
    base = step * CHUNK
    for cp in range(2):
        source = pl.multiple_of(base + cp * 384 + (1 - core) * LANES, LANES)
        target = pl.multiple_of((j * 4 + xh * 2 + cp) * LANES, LANES)
        peer_ref[:, pl.ds(target, LANES)] = block_ref[:, pl.ds(source, LANES)]
    source = pl.multiple_of(base + (1 - core) * 384 + 2 * LANES, LANES)
    target = pl.multiple_of((16 + j * 2 + xh) * LANES, LANES)
    peer_ref[:, pl.ds(target, LANES)] = block_ref[:, pl.ds(source, LANES)]


def preact_kernel(meta, tok_ref, w_ref, out_ref, peer_ref):
    out_ref[...] = jnp.zeros_like(out_ref)

    def body(pair, _):
        at = pl.ds(pl.multiple_of(pair * 2 * CHUNK, 2 * CHUNK), 2 * CHUNK)
        out_ref[...] += jnp.dot(tok_ref[:, at], w_ref[at, :], preferred_element_type=F32)
        for half in range(2):
            pack_columns(meta, pair * 2 + half, tok_ref, peer_ref)
        return 0

    lax.fori_loop(0, CHUNKS // 2, body, 0)


def hidden_kernel(meta, grad_ref, w_ref, preact_ref, hid_ref, peer_ref, acc_ref, slope_ref):
    acc_ref[...] = jnp.zeros_like(acc_ref)

    def body(pair, _):
        rows = pl.ds(pl.multiple_of(pair * LANES, LANES), LANES)
        preact = preact_ref[rows, :].T
        cumul = 0.5 * (1.0 + lax.erf(preact * (1.0 / math.sqrt(2.0))))
        density = jnp.exp(-0.5 * preact * preact) * (1.0 / math.sqrt(2.0 * math.pi))
        hid_ref[:, rows] = (preact * cumul).astype(BF16)
        slope_ref[:, rows] = cumul + preact * density
        at = pl.ds(pl.multiple_of(pair * 2 * CHUNK, 2 * CHUNK), 2 * CHUNK)
        acc_ref[...] += lax.dot_general(
            w_ref[:, at], grad_ref[:, at], (((1,), (1,)), ((), ())), preferred_element_type=F32
        )
        for half in range(2):
            pack_columns(meta, pair * 2 + half, grad_ref, peer_ref)
        return 0

    lax.fori_loop(0, CHUNKS // 2, body, 0)
    hid_ref[:, TOK : 2 * TOK] = (acc_ref[...] * slope_ref[...]).astype(BF16)


def term_kernel(meta, *refs, which, first):
    hid, hid_peer, full, peer = refs[:4]
    refs = refs[4 + (0 if first else 6) :]
    out_at = {0: (0, which), 1: (1, which), 3: (2, which), 2: (6, 0)}
    major = {d: refs[i].at[t] for d, (i, t) in out_at.items()}
    minor = {d: refs[i + (3 if d != 2 else 1)].at[t] for d, (i, t) in out_at.items()}
    scr = refs[8]
    core, own_x, own_y, own_z = meta[0], meta[1], meta[2], meta[3]
    lhs = slice((which == 1) * TOK, (which == 1) * TOK + TOK)

    def rows(x, y):
        return pl.ds(pl.multiple_of((x % 2) * 256 + y * SUB, SUB), SUB)

    def matmul(step, slot):
        tiles = []
        for q in range(4):
            if step < 4:
                group = (q // 2) * 8 + (own_z + step) % 4 * 2 + q % 2
                column = group * 384 + core * LANES
            else:
                group = (q % 2) * 8 + (own_z + (step - 4) * 2 + q // 2) % 4 * 2 + core
                column = group * 384 + 2 * LANES
            tiles.append(full[:, pl.ds(pl.multiple_of(column, LANES), LANES)])
        own = jnp.concatenate(tiles, axis=1)
        acc = jnp.dot(hid[:, lhs], own, preferred_element_type=F32)
        other = peer[:, step * 4 * LANES : (step + 1) * 4 * LANES]
        acc += jnp.dot(hid_peer[:, lhs], other, preferred_element_type=F32)
        acc = acc.astype(BF16)
        for q in range(4):
            scr[slot, q] = acc[:, q * LANES : (q + 1) * LANES]

    def scatter(step, slot):
        if step < 4:
            for d in range(4):
                for w in range(4):
                    x = (own_x + jnp.where(core == 0, d, w)) % 4
                    y = (own_y + jnp.where(core == 0, w, d)) % 4
                    for cp in range(2):
                        major[d][step, cp, w] = scr[slot, (x // 2) * 2 + cp, rows(x, y), :]
            return
        for jj in range(2):
            for xo in range(4):
                x = (own_x + xo) % 4
                for yo in range(4):
                    y = (own_y + yo) % 4
                    minor[(step - 4) * 2 + jj][xo, yo] = scr[slot, jj * 2 + x // 2, rows(x, y), :]

    matmul(0, 0)
    for step in range(1, 6):
        matmul(step, step % 2)
        scatter(step - 1, (step - 1) % 2)
    scatter(5, 1)


MAJOR1 = (4, 2, 4, SUB, LANES)
MINOR1 = (4, 4, SUB, LANES)


def bf16(*dims):
    return jax.ShapeDtypeStruct(dims, BF16)


def term_call(meta, which, hid, hid_peer, full, peer, buffers):
    operands = [meta, hid, hid_peer, full, peer]
    aliases = {}
    if buffers is not None:
        aliases = {len(operands) + i: i for i in range(6)}
        operands += list(buffers)
    return pl.pallas_call(
        functools.partial(term_kernel, which=which, first=buffers is None),
        in_specs=[SMEM] + [VMEM] * (len(operands) - 1),
        out_specs=[VMEM] * 8,
        out_shape=[bf16(2, *MAJOR1)] * 3 + [bf16(2, *MINOR1)] * 3 + [bf16(1, *MAJOR1), bf16(1, *MINOR1)],
        scratch_shapes=[pltpu.VMEM((2, 4, HID, LANES), BF16)],
        input_output_aliases=aliases,
        compiler_params=limit(LIM),
        cost_estimate=cost(4 * TOK * HID * HALF, 12 * 1024 * 1024),
    )(*operands)


def total(pieces):
    out = pieces[0].astype(F32)
    for piece in pieces[1:]:
        out += piece.astype(F32)
    return out


def major1_kernel(meta, *refs):
    core = meta[0]
    parts, two, out = refs[:3], refs[3:5], refs[5:9]
    for e in range(4):

        def body(f, _):
            j = jnp.where(core == 0, f, e)
            w = jnp.where(core == 0, e, f)
            for t in range(2):
                for cp in range(2):
                    pieces = [part[t, j, cp, w] for part in parts] + [two[t][0, j, cp, w]]
                    out[e][t, f, cp] = total(pieces).astype(BF16)
            return 0

        lax.fori_loop(0, 4, body, 0)


def minor1_kernel(meta, *refs):
    parts, two, out = refs[:3], refs[3:5], refs[6:10]
    for e in range(4):

        def body(f, _):
            for t in range(2):
                pieces = [part[t, e, f] for part in parts] + [two[t][0, e, f]]
                out[e][t, f] = total(pieces).astype(BF16)
            return 0

        lax.fori_loop(0, 4, body, 0)


def major2_kernel(meta, *refs):
    parts, out = refs[:4], refs[5:9]
    for f in range(4):
        for t in range(2):
            for cp in range(2):
                out[f][t, cp] = total([part[t, f, cp] for part in parts]).astype(BF16)


def minor2_kernel(meta, *refs):
    parts, out = refs[:4], refs[5:9]
    for f in range(4):
        for t in range(2):
            out[f][t] = total([part[t, f] for part in parts]).astype(BF16)


def major3_kernel(meta, *refs):
    parts, (keep, send) = refs[:4], refs[5:7]
    core = meta[0]
    for t in range(2):
        keep[t] = total([part[t, core] for part in parts])
        send[t] = total([part[t, 1 - core] for part in parts])


def final_kernel(meta, keep, got, p0, p1, p2, p3, up_ref, down_ref, *, factor):
    first = meta[0] == 0
    for t, out in ((0, down_ref), (1, up_ref)):
        out[:, 0:LANES] = jnp.where(first, keep[t], got[t]) * factor
        out[:, LANES : 2 * LANES] = jnp.where(first, got[t], keep[t]) * factor
        out[:, 2 * LANES : 3 * LANES] = total([part[t] for part in (p0, p1, p2, p3)]) * factor


def sum_call(kernel, meta, operands, shapes, after=None):
    in_specs = [SMEM] + [VMEM] * len(operands)
    operands = [meta, *operands]
    if after is not None:
        in_specs.append(ANY)
        operands.append(after)
    return pl.pallas_call(
        kernel,
        in_specs=in_specs,
        out_specs=[VMEM] * len(shapes),
        out_shape=shapes,
        compiler_params=limit(LIM),
    )(*operands)


def ring(parts, axis0, axis1):
    return [parts[0]] + [shift(parts[d], axis0, axis1, d) for d in (2, 1, 3)]


def local(tokens, grad_out, w_up, w_down):
    index = lax.axis_index(AXES)
    place = jnp.arange(4, dtype=jnp.int32)
    xh, z, core = index // 64, (index // 16) % 4, (index // 8) % 2
    xl, y = (index // 4) % 2, index % 4
    meta = jnp.where(place == 0, core, jnp.where(place == 1, xh * 2 + xl, jnp.where(place == 2, y, z)))
    meta = meta.astype(jnp.int32)

    preact, pack_tok = pl.pallas_call(
        preact_kernel,
        in_specs=[SMEM, VMEM, VMEM],
        out_specs=[VMEM] * 2,
        out_shape=[jax.ShapeDtypeStruct((TOK, HID), F32), bf16(TOK, HALF)],
        compiler_params=limit(LIM),
        cost_estimate=cost(2 * TOK * HID * WIDTH, 16 * 1024 * 1024),
        name="preact",
    )(meta, tokens, w_up)
    peer_tok = swap(pack_tok)

    hid, pack_grad = pl.pallas_call(
        hidden_kernel,
        in_specs=[SMEM, VMEM, VMEM, VMEM],
        out_specs=[VMEM] * 2,
        out_shape=[bf16(HID, 2 * TOK), bf16(TOK, HALF)],
        scratch_shapes=[pltpu.VMEM((HID, TOK), F32), pltpu.VMEM((HID, TOK), F32)],
        compiler_params=limit(LIM),
        cost_estimate=cost(2 * TOK * HID * WIDTH, 18 * 1024 * 1024),
        name="hidden",
    )(meta, grad_out, w_down, preact)
    hid_peer = swap(hid)
    peer_grad = swap(pack_grad)

    out = term_call(meta, 1, hid, hid_peer, tokens, peer_tok, None)
    major_up = shift(out[6], "x", "y", 2)
    minor_up = shift(out[7], "z", "z", 2)
    out = term_call(meta, 0, hid, hid_peer, grad_out, peer_grad, out[:6])

    major_two = [shift(out[6], "x", "y", 2), major_up]
    minor_two = [shift(out[7], "z", "z", 2), minor_up]
    major = [out[0], shift(out[1], "x", "y", 1), shift(out[2], "x", "y", 3)]
    minor = [out[3], shift(out[4], "z", "z", 1), shift(out[5], "z", "z", 3)]
    major = sum_call(major1_kernel, meta, major + major_two, [bf16(2, 4, 2, SUB, LANES)] * 4)
    minor = sum_call(minor1_kernel, meta, minor + minor_two, [bf16(2, 4, SUB, LANES)] * 4, major[0])
    major = ring(major, "y", "z")
    last = minor[0]
    minor = ring(minor, "x", "x")
    major = sum_call(major2_kernel, meta, major, [bf16(2, 2, SUB, LANES)] * 4, last)
    minor = sum_call(minor2_kernel, meta, minor, [bf16(2, SUB, LANES)] * 4, major[0])
    major = ring(major, "z", "x")
    last = minor[0]
    minor = ring(minor, "y", "y")
    keep, send = sum_call(
        major3_kernel, meta, major, [jax.ShapeDtypeStruct((2, SUB, LANES), F32)] * 2, last
    )
    total_tokens = tokens.shape[0] * lax.axis_size("row") * lax.axis_size("col")
    up, down = sum_call(
        functools.partial(final_kernel, factor=1.0 / math.sqrt(total_tokens)),
        meta, [keep, swap(send)] + minor,
        [jax.ShapeDtypeStruct((SUB, COLORS * LANES), F32)] * 2,
    )
    return up.T, down.T


def solution(mesh):
    placed = (P(AXES, None), P(AXES, None), P(), P())
    return jax.shard_map(
        local,
        mesh=mesh,
        in_specs=placed,
        out_specs=(P("row", "col"), P("row", "col")),
        check_vma=False,
    )
```

time: 202 us -> 112 us (0.55)
  the two profiles are of different devices: /device:TPU:17 before, /device:TPU:24 now
where the time goes in v1:
time: 112 us
  waiting for transfers between devices  47.8 us (43%)
  starting transfers between devices  32.6 us (29%)
  Pallas kernels  25 us (22%)
  local copies, waits for them, and re-layouts  5.72 us (5%)
    ppermute x20, waiting for transfers between devices, shift(): return lax.ppermute(value, AXES, pairs)  41.1 us
    ppermute x20, starting transfers between devices, shift(): return lax.ppermute(value, AXES, pairs)  31.8 us
    pallas_call x2, Pallas kernels, term_call(): pl.pallas_call(functools.partial(term_kernel, which=which, first=buffers...  8.82 us
    ppermute x4, waiting for transfers between devices, swap(): return lax.ppermute(value, AXES, pairs)  6.7 us
    unnamed x14, local copies, waits for them, and re-layouts  5.72 us
    pallas_call x1, Pallas kernels, local(): pl.pallas_call(hidden_kernel, in_specs=[SMEM, VMEM, VMEM, VMEM], out_spec...  5.68 us
    pallas_call x1, Pallas kernels, local(): pl.pallas_call(preact_kernel, in_specs=[SMEM, VMEM, VMEM], out_specs=[VME...  5.37 us
    pallas_call x6, Pallas kernels, sum_call(): pl.pallas_call(kernel, in_specs=in_specs, out_specs=[VMEM] * len(shapes),...  5.16 us
  transfers between devices with their start and end apart: 24, of which 11 were waited for; matrix products, arithmetic and copies ran while one was open for 0% of the time, Pallas kernels for 12%

profile of v1, /device:TPU:24, one launch (start us, length us, event | category | flops | bytes accessed | tf_op | source)
XLA Modules:
  0.0 112.1 jit_solution(857487617799402111)
XLA Ops:
  0.6 0.0 slice-start
  0.8 2.9 %copy-done = bf16[6144,512]{1,0:T(8,128)(2,1)S(1)} copy-done((bf16[6144,512]{1,0:T(8,128)(2,1)S(1)}, bf16[6144,512]{1,0:T(8,128)(2,1)}, u32[]{:S(2)}) %copy-start) | copy-done | bytes 6291480
  3.7 2.8 %copy-done.2 = bf16[512,6144]{1,0:T(8,128)(2,1)S(1)} copy-done((bf16[512,6144]{1,0:T(8,128)(2,1)S(1)}, bf16[512,6144]{1,0:T(8,128)(2,1)}, u32[]{:S(2)}) %copy-start.2) | copy-done | bytes 6291480
  6.5 5.4 %preact.1 = (f32[512,512]{1,0:T(8,128)S(1)}, bf16[512,3072]{1,0:T(8,128)(2,1)S(1)}) custom-call(s32[4]{0:T(128)S(1)} %compare_select_fusion.2.meta, bf16[512,6144]{1,0:T(8,128)(2,1)S(1)} %copy-done.2, bf16[6144,512]{1,0:T(8,128)(2,1)S(1)} %copy-done), custom_call_target="tpu_custom_call" | custom-call | flops 3221225472 | bytes 16777216 | tf_op jit(solution)/shard_map/preact/pallas_call | solution.py:295
  11.8 0.1 collective-permute-start.2
  12.0 0.0 slice-start.3
  12.0 5.7 %hidden.1 = (bf16[512,1024]{1,0:T(8,128)(2,1)S(1)}, bf16[512,3072]{1,0:T(8,128)(2,1)S(1)}) custom-call(s32[4]{0:T(128)S(1)} %compare_select_fusion.2.meta, bf16[512,6144]{1,0:T(8,128)(2,1)S(1)} %bitcast.3, bf16[512,6144]{1,0:T(8,128)(2,1)S(1)} %copy-done.1, f32[512,512]{1,0:T(8,128)S(1)} %get-tuple-element.42.preact_ref), custom_call_target="tpu_custom_call" | custom-call | flops 3221225472 | bytes 18874368 | tf_op jit(solution)/shard_map/hidden/pallas_call | solution.py:306
  17.7 0.6 collective-permute-start.1
  18.3 0.1 collective-permute-start
  18.3 6.7 %collective-permute-done.refs_1_ = bf16[512,1024]{1,0:T(8,128)(2,1)S(1)} collective-permute-done((bf16[512,1024]{1,0:T(8,128)(2,1)S(1)}, bf16[512,1024]{1,0:T(8,128)(2,1)S(1)}, u32[]{:S(2)}, u32[]{:S(2)}) %collective-permute-start) | collective-permute-done | bytes 1048608 | tf_op jit(solution)/shard_map/ppermute | solution.py:52
  25.1 4.4 %shard_map.59 = (bf16[2,4,2,4,64,128]{5,4,3,2,1,0:T(8,128)(2,1)S(1)}, bf16[2,4,2,4,64,128]{5,4,3,2,1,0:T(8,128)(2,1)S(1)}, bf16[2,4,2,4,64,128]{5,4,3,2,1,0:T(8,...) custom-call(s32[4]{0:T(128)S(1)} %compare_select_fusion.2.meta, ...), custom_call_target="tpu_custom_call" | custom-call | flops 3221225472 | bytes 12582912 | tf_op jit(solution)/shard_map/pallas_call | solution.py:188
  29.5 4.4 %shard_map.60 = (bf16[2,4,2,4,64,128]{5,4,3,2,1,0:T(8,128)(2,1)S(1)}, bf16[2,4,2,4,64,128]{5,4,3,2,1,0:T(8,128)(2,1)S(1)}, bf16[2,4,2,4,64,128]{5,4,3,2,1,0:T(8,...) custom-call(s32[4]{0:T(128)S(1)} %compare_select_fusion.2.meta, ...), custom_call_target="tpu_custom_call", output_to_operand_aliasing={{0}: (5, {}), {1}: (6, {}), {2}: (7, {}), {3}: (8, {}), {4}... | custom-call | flops 3221225472 | bytes 12582912 | tf_op jit(solution)/shard_map/pallas_call | solution.py:188
  33.9 1.6 %collective-permute-start.3 = (bf16[2,4,2,4,64,128]{5,4,3,2,1,0:T(8,128)(2,1)S(1)}, bf16[2,4,2,4,64,128]{5,4,3,2,1,0:T(8,128)(2,1)S(1)}, u32[]{:S(2)}, u32[]{:S(2)}) collective-permute-start(bf16[2,4,2,4,64,128]{5,4,3,2,1,0:T(8,128)(2,1)S(1)} %get-tuple-element.53), channel_id=1, source_target_pairs={{0,4},{1,5},{2,6},{3,7},{4,64},{5,65},{6,66},{7,67},{8,9},{9,10},{... | collective-permute-start | bytes 3145736 | tf_op jit(solution)/shard_map/ppermute | solution.py:44
  35.5 1.7 %collective-permute-start.4 = (bf16[2,4,2,4,64,128]{5,4,3,2,1,0:T(8,128)(2,1)S(1)}, bf16[2,4,2,4,64,128]{5,4,3,2,1,0:T(8,128)(2,1)S(1)}, u32[]{:S(2)}, u32[]{:S(2)}) collective-permute-start(bf16[2,4,2,4,64,128]{5,4,3,2,1,0:T(8,128)(2,1)S(1)} %get-tuple-element.54), channel_id=1, source_target_pairs={{0,68},{1,69},{2,70},{3,71},{4,0},{5,1},{6,2},{7,3},{8,11},{9,8},{... | collective-permute-start | bytes 3145736 | tf_op jit(solution)/shard_map/ppermute | solution.py:44
  37.2 1.8 %collective-permute-start.5 = (bf16[1,4,2,4,64,128]{5,4,3,2,1,0:T(8,128)(2,1)S(1)}, bf16[1,4,2,4,64,128]{5,4,3,2,1,0:T(8,128)(2,1)S(1)}, u32[]{:S(2)}, u32[]{:S(2)}) collective-permute-start(bf16[1,4,2,4,64,128]{5,4,3,2,1,0:T(8,128)(2,1)S(1)} %get-tuple-element.55), channel_id=1, source_target_pairs={{0,64},{1,65},{2,66},{3,67},{4,68},{5,69},{6,70},{7,71},{8,10},{9,... | collective-permute-start | bytes 1572872 | tf_op jit(solution)/shard_map/ppermute | solution.py:44
  39.0 1.7 %collective-permute-start.6 = (bf16[1,4,2,4,64,128]{5,4,3,2,1,0:T(8,128)(2,1)S(1)}, bf16[1,4,2,4,64,128]{5,4,3,2,1,0:T(8,128)(2,1)S(1)}, u32[]{:S(2)}, u32[]{:S(2)}) collective-permute-start(bf16[1,4,2,4,64,128]{5,4,3,2,1,0:T(8,128)(2,1)S(1)} %get-tuple-element.56), channel_id=1, source_target_pairs={{0,64},{1,65},{2,66},{3,67},{4,68},{5,69},{6,70},{7,71},{8,10},{9,... | collective-permute-start | bytes 1572872 | tf_op jit(solution)/shard_map/ppermute | solution.py:44
  40.7 1.8 %collective-permute-start.10 = (bf16[2,4,4,64,128]{4,3,2,1,0:T(8,128)(2,1)S(1)}, bf16[2,4,4,64,128]{4,3,2,1,0:T(8,128)(2,1)S(1)}, u32[]{:S(2)}, u32[]{:S(2)}) collective-permute-start(bf16[2,4,4,64,128]{4,3,2,1,0:T(8,128)(2,1)S(1)} %get-tuple-element.62), channel_id=1, source_target_pairs={{0,16},{1,17},{2,18},{3,19},{4,20},{5,21},{6,22},{7,23},{8,24},{9,... | collective-permute-start | bytes 1572872 | tf_op jit(solution)/shard_map/ppermute | solution.py:44
  42.6 14.0 %collective-permute-done.5.refs_3_ = bf16[1,4,2,4,64,128]{5,4,3,2,1,0:T(8,128)(2,1)S(1)} collective-permute-done((bf16[1,4,2,4,64,128]{5,4,3,2,1,0:T(8,128)(2,1)S(1)}, bf16[1,4,2,4,64,128]{5,4,3,2,1,0:T(8,128)(2,1)S(1)}, u32[]{:S(2)}, u32[]{:S(2)}) %collective-permute-start.5) | collective-permute-done | bytes 524320 | tf_op jit(solution)/shard_map/ppermute | solution.py:44
  56.6 4.0 %collective-permute-start.11 = (bf16[2,4,4,64,128]{4,3,2,1,0:T(8,128)(2,1)S(1)}, bf16[2,4,4,64,128]{4,3,2,1,0:T(8,128)(2,1)S(1)}, u32[]{:S(2)}, u32[]{:S(2)}) collective-permute-start(bf16[2,4,4,64,128]{4,3,2,1,0:T(8,128)(2,1)S(1)} %get-tuple-element.63), channel_id=1, source_target_pairs={{0,48},{1,49},{2,50},{3,51},{4,52},{5,53},{6,54},{7,55},{8,56},{9,... | collective-permute-start | bytes 1572872 | tf_op jit(solution)/shard_map/ppermute | solution.py:44
  60.5 1.7 %collective-permute-done.6.refs_4_ = bf16[1,4,2,4,64,128]{5,4,3,2,1,0:T(8,128)(2,1)S(1)} collective-permute-done((bf16[1,4,2,4,64,128]{5,4,3,2,1,0:T(8,128)(2,1)S(1)}, bf16[1,4,2,4,64,128]{5,4,3,2,1,0:T(8,128)(2,1)S(1)}, u32[]{:S(2)}, u32[]{:S(2)}) %collective-permute-start.6) | collective-permute-done | bytes 524320 | tf_op jit(solution)/shard_map/ppermute | solution.py:44
  62.2 3.8 %collective-permute-start.12 = (bf16[1,4,4,64,128]{4,3,2,1,0:T(8,128)(2,1)S(1)}, bf16[1,4,4,64,128]{4,3,2,1,0:T(8,128)(2,1)S(1)}, u32[]{:S(2)}, u32[]{:S(2)}) collective-permute-start(bf16[1,4,4,64,128]{4,3,2,1,0:T(8,128)(2,1)S(1)} %get-tuple-element.64), channel_id=1, source_target_pairs={{0,32},{1,33},{2,34},{3,35},{4,36},{5,37},{6,38},{7,39},{8,40},{9,... | collective-permute-start | bytes 786440 | tf_op jit(solution)/shard_map/ppermute | solution.py:44
  66.0 0.0 collective-permute-start.13
  66.1 1.2 %shard_map.61 = (bf16[2,4,2,64,128]{4,3,2,1,0:T(8,128)(2,1)S(1)}, bf16[2,4,2,64,128]{4,3,2,1,0:T(8,128)(2,1)S(1)}, bf16[2,4,2,64,128]{4,3,2,1,0:T(8,128)(2,1)S(1)}, bf16[2,4,2,64,128]{4,3,2,1,0:T(8,128)(2,1)S(1)}) custom-call(s32[4]{0:T(128)S(1)} %compare_select_fusion.2.meta, bf16[2,4,2,4,64,128]{5,4,3,2,1,0:T(8,128)(2,1)S(1)} %get-tuple-element.52.refs_0_, ...), custom_call_target="tpu_custom_call" | custom-call | tf_op jit(solution)/shard_map/pallas_call | solution.py:274
  67.2 1.3 %collective-permute-start.7 = (bf16[2,4,2,64,128]{4,3,2,1,0:T(8,128)(2,1)S(1)}, bf16[2,4,2,64,128]{4,3,2,1,0:T(8,128)(2,1)S(1)}, u32[]{:S(2)}, u32[]{:S(2)}) collective-permute-start(bf16[2,4,2,64,128]{4,3,2,1,0:T(8,128)(2,1)S(1)} %get-tuple-element.58), channel_id=1, source_target_pairs={{0,2},{1,3},{2,0},{3,1},{4,6},{5,7},{6,4},{7,5},{8,40},{9,41},{10,... | collective-permute-start | bytes 786440 | tf_op jit(solution)/shard_map/ppermute | solution.py:44
  68.6 4.6 %collective-permute-done.12.refs_3_ = bf16[1,4,4,64,128]{4,3,2,1,0:T(8,128)(2,1)S(1)} collective-permute-done((bf16[1,4,4,64,128]{4,3,2,1,0:T(8,128)(2,1)S(1)}, bf16[1,4,4,64,128]{4,3,2,1,0:T(8,128)(2,1)S(1)}, u32[]{:S(2)}, u32[]{:S(2)}) %collective-permute-start.12) | collective-permute-done | bytes 262176 | tf_op jit(solution)/shard_map/ppermute | solution.py:44
  73.2 0.2 collective-permute-start.8
  73.4 5.5 %collective-permute-done.13.refs_4_ = bf16[1,4,4,64,128]{4,3,2,1,0:T(8,128)(2,1)S(1)} collective-permute-done((bf16[1,4,4,64,128]{4,3,2,1,0:T(8,128)(2,1)S(1)}, bf16[1,4,4,64,128]{4,3,2,1,0:T(8,128)(2,1)S(1)}, u32[]{:S(2)}, u32[]{:S(2)}) %collective-permute-start.13) | collective-permute-done | bytes 262176 | tf_op jit(solution)/shard_map/ppermute | solution.py:44
  78.9 0.7 collective-permute-start.9
  79.6 7.0 %collective-permute-done.11.refs_2_ = bf16[2,4,4,64,128]{4,3,2,1,0:T(8,128)(2,1)S(1)} collective-permute-done((bf16[2,4,4,64,128]{4,3,2,1,0:T(8,128)(2,1)S(1)}, bf16[2,4,4,64,128]{4,3,2,1,0:T(8,128)(2,1)S(1)}, u32[]{:S(2)}, u32[]{:S(2)}) %collective-permute-start.11) | collective-permute-done | bytes 524320 | tf_op jit(solution)/shard_map/ppermute | solution.py:44
  86.6 0.9 shard_map.62
  87.5 1.2 %collective-permute-start.17 = (bf16[2,4,64,128]{3,2,1,0:T(8,128)(2,1)S(1)}, bf16[2,4,64,128]{3,2,1,0:T(8,128)(2,1)S(1)}, u32[]{:S(2)}, u32[]{:S(2)}) collective-permute-start(bf16[2,4,64,128]{3,2,1,0:T(8,128)(2,1)S(1)} %get-tuple-element.71), channel_id=1, source_target_pairs={{0,64},{1,65},{2,66},{3,67},{4,68},{5,69},{6,70},{7,71},{8,72},{9,... | collective-permute-start | bytes 393224 | tf_op jit(solution)/shard_map/ppermute | solution.py:44
  88.7 2.1 %collective-permute-start.18 = (bf16[2,4,64,128]{3,2,1,0:T(8,128)(2,1)S(1)}, bf16[2,4,64,128]{3,2,1,0:T(8,128)(2,1)S(1)}, u32[]{:S(2)}, u32[]{:S(2)}) collective-permute-start(bf16[2,4,64,128]{3,2,1,0:T(8,128)(2,1)S(1)} %get-tuple-element.72), channel_id=1, source_target_pairs={{0,4},{1,5},{2,6},{3,7},{4,64},{5,65},{6,66},{7,67},{8,12},{9,13},... | collective-permute-start | bytes 393224 | tf_op jit(solution)/shard_map/ppermute | solution.py:44
  90.8 1.1 %collective-permute-start.19 = (bf16[2,4,64,128]{3,2,1,0:T(8,128)(2,1)S(1)}, bf16[2,4,64,128]{3,2,1,0:T(8,128)(2,1)S(1)}, u32[]{:S(2)}, u32[]{:S(2)}) collective-permute-start(bf16[2,4,64,128]{3,2,1,0:T(8,128)(2,1)S(1)} %get-tuple-element.73), channel_id=1, source_target_pairs={{0,68},{1,69},{2,70},{3,71},{4,0},{5,1},{6,2},{7,3},{8,76},{9,77},... | collective-permute-start | bytes 393224 | tf_op jit(solution)/shard_map/ppermute | solution.py:44
  91.9 0.7 shard_map.63
  92.6 0.1 collective-permute-start.14
  92.7 4.5 %collective-permute-start.15 = (bf16[2,2,64,128]{3,2,1,0:T(8,128)(2,1)S(1)}, bf16[2,2,64,128]{3,2,1,0:T(8,128)(2,1)S(1)}, u32[]{:S(2)}, u32[]{:S(2)}) collective-permute-start(bf16[2,2,64,128]{3,2,1,0:T(8,128)(2,1)S(1)} %get-tuple-element.69), channel_id=1, source_target_pairs={{0,16},{1,17},{2,18},{3,19},{4,20},{5,21},{6,22},{7,23},{8,12},{9,... | collective-permute-start | bytes 196616 | tf_op jit(solution)/shard_map/ppermute | solution.py:44
  97.3 0.5 collective-permute-start.16
  97.8 0.6 shard_map.64
  98.4 0.1 collective-permute-done.14.refs_1_
  98.5 0.7 collective-permute-done.15.refs_2_
  99.2 2.3 %collective-permute-done.16.refs_3_ = bf16[2,2,64,128]{3,2,1,0:T(8,128)(2,1)S(1)} collective-permute-done((bf16[2,2,64,128]{3,2,1,0:T(8,128)(2,1)S(1)}, bf16[2,2,64,128]{3,2,1,0:T(8,128)(2,1)S(1)}, u32[]{:S(2)}, u32[]{:S(2)}) %collective-permute-start.16) | collective-permute-done | bytes 65568 | tf_op jit(solution)/shard_map/ppermute | solution.py:44
  101.5 0.6 shard_map.65
  102.1 0.1 collective-permute-start.20
  102.2 1.3 %collective-permute-start.21 = (bf16[2,64,128]{2,1,0:T(8,128)(2,1)S(1)}, bf16[2,64,128]{2,1,0:T(8,128)(2,1)S(1)}, u32[]{:S(2)}, u32[]{:S(2)}) collective-permute-start(bf16[2,64,128]{2,1,0:T(8,128)(2,1)S(1)} %get-tuple-element.77), channel_id=1, source_target_pairs={{0,2},{1,3},{2,0},{3,1},{4,6},{5,7},{6,4},{7,5},{8,10},{9,11},{10,... | collective-permute-start | bytes 98312 | tf_op jit(solution)/shard_map/ppermute | solution.py:44
  103.5 2.2 %collective-permute-start.22 = (bf16[2,64,128]{2,1,0:T(8,128)(2,1)S(1)}, bf16[2,64,128]{2,1,0:T(8,128)(2,1)S(1)}, u32[]{:S(2)}, u32[]{:S(2)}) collective-permute-start(bf16[2,64,128]{2,1,0:T(8,128)(2,1)S(1)} %get-tuple-element.78), channel_id=1, source_target_pairs={{0,1},{1,2},{2,3},{3,0},{4,5},{5,6},{6,7},{7,4},{8,9},{9,10},{10,1... | collective-permute-start | bytes 98312 | tf_op jit(solution)/shard_map/ppermute | solution.py:44
  105.7 2.0 %collective-permute-done.21.p1 = bf16[2,64,128]{2,1,0:T(8,128)(2,1)S(1)} collective-permute-done((bf16[2,64,128]{2,1,0:T(8,128)(2,1)S(1)}, bf16[2,64,128]{2,1,0:T(8,128)(2,1)S(1)}, u32[]{:S(2)}, u32[]{:S(2)}) %collective-permute-start.21) | collective-permute-done | bytes 32800 | tf_op jit(solution)/shard_map/ppermute | solution.py:44
  107.7 3.1 %collective-permute-done.23.p3 = bf16[2,64,128]{2,1,0:T(8,128)(2,1)S(1)} collective-permute-done((bf16[2,64,128]{2,1,0:T(8,128)(2,1)S(1)}, bf16[2,64,128]{2,1,0:T(8,128)(2,1)S(1)}, u32[]{:S(2)}, u32[]{:S(2)}) %collective-permute-start.23) | collective-permute-done | bytes 32800 | tf_op jit(solution)/shard_map/ppermute | solution.py:44
  110.8 1.2 %shard_map.66 = (f32[64,384]{1,0:T(8,128)}, f32[64,384]{1,0:T(8,128)}) custom-call(s32[4]{0:T(128)S(1)} %compare_select_fusion.2.meta, f32[2,64,128]{2,1,0:T(8,128)S(1)} %get-tuple-element.75.keep, f32[2,64,128]{2,1,0:T(8,128)S(1)} %collective-permute-done.20.got, bf16[2,64,128]{2,1,0:T(8,128)(2,1)S(1)} %get-tuple-element.74.refs_4_.p0, ...), custom_call_target="tpu_custom_call" | custom-call | tf_op jit(solution)/shard_map/pallas_call | solution.py:274
  (27 shorter events, 0.1 us)
Async XLA Ops:
  0.6 11.3 %slice-start = ((s8[6291456]{0:T(1024)(128)(4,1)}), s8[2097152]{0:T(1024)(128)(4,1)S(1)}, s32[]{:S(2)}) async-start(s8[6291456]{0:T(1024)(128)(4,1)} %bitcast.2), calls=%async_computation | async-start | bytes 4194304
  0.7 2.9 %copy-start = (bf16[6144,512]{1,0:T(8,128)(2,1)S(1)}, bf16[6144,512]{1,0:T(8,128)(2,1)}, u32[]{:S(2)}) copy-start(bf16[6144,512]{1,0:T(8,128)(2,1)} %w_ref.2) | copy-start | bytes 18874372
  3.7 2.8 %copy-start.2 = (bf16[512,6144]{1,0:T(8,128)(2,1)S(1)}, bf16[512,6144]{1,0:T(8,128)(2,1)}, u32[]{:S(2)}) copy-start(bf16[512,6144]{1,0:T(8,128)(2,1)} %refs_2_.2) | copy-start | bytes 18874372
  6.5 5.5 %slice-start.1 = ((s8[6291456]{0:T(1024)(128)(4,1)}), s8[4194304]{0:T(1024)(128)(4,1)S(1)}, s32[]{:S(2)}) async-start(s8[6291456]{0:T(1024)(128)(4,1)} %bitcast.2), calls=%async_computation.1 | async-start | bytes 8388608
  6.5 5.5 %copy-start.1 = (bf16[512,6144]{1,0:T(8,128)(2,1)S(1)}, bf16[512,6144]{1,0:T(8,128)(2,1)}, u32[]{:S(2)}) copy-start(bf16[512,6144]{1,0:T(8,128)(2,1)} %w_ref.3) | copy-start | bytes 18874372
  6.5 18.6 %slice-start.2 = ((s8[6291456]{0:T(1024)(128)(4,1)}), s8[4194304]{0:T(1024)(128)(4,1)S(1)}, s32[]{:S(2)}) async-start(s8[6291456]{0:T(1024)(128)(4,1)} %bitcast.4), calls=%async_computation.2 | async-start | bytes 8388608
  11.8 13.2 %collective-permute-start.2 = (bf16[512,3072]{1,0:T(8,128)(2,1)S(1)}, bf16[512,3072]{1,0:T(8,128)(2,1)S(1)}, u32[]{:S(2)}, u32[]{:S(2)}) collective-permute-start(bf16[512,3072]{1,0:T(8,128)(2,1)S(1)} %get-tuple-element.45), channel_id=1, source_target_pairs={{0,8},{1,9},{2,10},{3,11},{4,12},{5,13},{6,14},{7,15},{8,0},{9,1},... | collective-permute-start | bytes 9437192 | tf_op jit(solution)/shard_map/ppermute | solution.py:52
  12.0 13.1 %slice-start.3 = ((s8[6291456]{0:T(1024)(128)(4,1)}), s8[2097152]{0:T(1024)(128)(4,1)S(1)}, s32[]{:S(2)}) async-start(s8[6291456]{0:T(1024)(128)(4,1)} %bitcast.4), calls=%async_computation.3 | async-start | bytes 4194304
  17.7 11.8 %collective-permute-start.1 = (bf16[512,3072]{1,0:T(8,128)(2,1)S(1)}, bf16[512,3072]{1,0:T(8,128)(2,1)S(1)}, u32[]{:S(2)}, u32[]{:S(2)}) collective-permute-start(bf16[512,3072]{1,0:T(8,128)(2,1)S(1)} %get-tuple-element.44), channel_id=1, source_target_pairs={{0,8},{1,9},{2,10},{3,11},{4,12},{5,13},{6,14},{7,15},{8,0},{9,1},... | collective-permute-start | bytes 9437192 | tf_op jit(solution)/shard_map/ppermute | solution.py:52
  18.3 6.8 %collective-permute-start = (bf16[512,1024]{1,0:T(8,128)(2,1)S(1)}, bf16[512,1024]{1,0:T(8,128)(2,1)S(1)}, u32[]{:S(2)}, u32[]{:S(2)}) collective-permute-start(bf16[512,1024]{1,0:T(8,128)(2,1)S(1)} %get-tuple-element.43.refs_0_), channel_id=1, source_target_pairs={{0,8},{1,9},{2,10},{3,11},{4,12},{5,13},{6,14},{7,15},{8,0},{9,1},... | collective-permute-start | bytes 3145736 | tf_op jit(solution)/shard_map/ppermute | solution.py:52
  33.9 32.1 %collective-permute-start.3 = (bf16[2,4,2,4,64,128]{5,4,3,2,1,0:T(8,128)(2,1)S(1)}, bf16[2,4,2,4,64,128]{5,4,3,2,1,0:T(8,128)(2,1)S(1)}, u32[]{:S(2)}, u32[]{:S(2)}) collective-permute-start(bf16[2,4,2,4,64,128]{5,4,3,2,1,0:T(8,128)(2,1)S(1)} %get-tuple-element.53), channel_id=1, source_target_pairs={{0,4},{1,5},{2,6},{3,7},{4,64},{5,65},{6,66},{7,67},{8,9},{9,10},{... | collective-permute-start | bytes 3145736 | tf_op jit(solution)/shard_map/ppermute | solution.py:44
  35.5 30.6 %collective-permute-start.4 = (bf16[2,4,2,4,64,128]{5,4,3,2,1,0:T(8,128)(2,1)S(1)}, bf16[2,4,2,4,64,128]{5,4,3,2,1,0:T(8,128)(2,1)S(1)}, u32[]{:S(2)}, u32[]{:S(2)}) collective-permute-start(bf16[2,4,2,4,64,128]{5,4,3,2,1,0:T(8,128)(2,1)S(1)} %get-tuple-element.54), channel_id=1, source_target_pairs={{0,68},{1,69},{2,70},{3,71},{4,0},{5,1},{6,2},{7,3},{8,11},{9,8},{... | collective-permute-start | bytes 3145736 | tf_op jit(solution)/shard_map/ppermute | solution.py:44
  37.2 19.4 %collective-permute-start.5 = (bf16[1,4,2,4,64,128]{5,4,3,2,1,0:T(8,128)(2,1)S(1)}, bf16[1,4,2,4,64,128]{5,4,3,2,1,0:T(8,128)(2,1)S(1)}, u32[]{:S(2)}, u32[]{:S(2)}) collective-permute-start(bf16[1,4,2,4,64,128]{5,4,3,2,1,0:T(8,128)(2,1)S(1)} %get-tuple-element.55), channel_id=1, source_target_pairs={{0,64},{1,65},{2,66},{3,67},{4,68},{5,69},{6,70},{7,71},{8,10},{9,... | collective-permute-start | bytes 1572872 | tf_op jit(solution)/shard_map/ppermute | solution.py:44
  39.0 23.2 %collective-permute-start.6 = (bf16[1,4,2,4,64,128]{5,4,3,2,1,0:T(8,128)(2,1)S(1)}, bf16[1,4,2,4,64,128]{5,4,3,2,1,0:T(8,128)(2,1)S(1)}, u32[]{:S(2)}, u32[]{:S(2)}) collective-permute-start(bf16[1,4,2,4,64,128]{5,4,3,2,1,0:T(8,128)(2,1)S(1)} %get-tuple-element.56), channel_id=1, source_target_pairs={{0,64},{1,65},{2,66},{3,67},{4,68},{5,69},{6,70},{7,71},{8,10},{9,... | collective-permute-start | bytes 1572872 | tf_op jit(solution)/shard_map/ppermute | solution.py:44
  40.7 38.9 %collective-permute-start.10 = (bf16[2,4,4,64,128]{4,3,2,1,0:T(8,128)(2,1)S(1)}, bf16[2,4,4,64,128]{4,3,2,1,0:T(8,128)(2,1)S(1)}, u32[]{:S(2)}, u32[]{:S(2)}) collective-permute-start(bf16[2,4,4,64,128]{4,3,2,1,0:T(8,128)(2,1)S(1)} %get-tuple-element.62), channel_id=1, source_target_pairs={{0,16},{1,17},{2,18},{3,19},{4,20},{5,21},{6,22},{7,23},{8,24},{9,... | collective-permute-start | bytes 1572872 | tf_op jit(solution)/shard_map/ppermute | solution.py:44
  56.6 30.0 %collective-permute-start.11 = (bf16[2,4,4,64,128]{4,3,2,1,0:T(8,128)(2,1)S(1)}, bf16[2,4,4,64,128]{4,3,2,1,0:T(8,128)(2,1)S(1)}, u32[]{:S(2)}, u32[]{:S(2)}) collective-permute-start(bf16[2,4,4,64,128]{4,3,2,1,0:T(8,128)(2,1)S(1)} %get-tuple-element.63), channel_id=1, source_target_pairs={{0,48},{1,49},{2,50},{3,51},{4,52},{5,53},{6,54},{7,55},{8,56},{9,... | collective-permute-start | bytes 1572872 | tf_op jit(solution)/shard_map/ppermute | solution.py:44
  62.2 11.0 %collective-permute-start.12 = (bf16[1,4,4,64,128]{4,3,2,1,0:T(8,128)(2,1)S(1)}, bf16[1,4,4,64,128]{4,3,2,1,0:T(8,128)(2,1)S(1)}, u32[]{:S(2)}, u32[]{:S(2)}) collective-permute-start(bf16[1,4,4,64,128]{4,3,2,1,0:T(8,128)(2,1)S(1)} %get-tuple-element.64), channel_id=1, source_target_pairs={{0,32},{1,33},{2,34},{3,35},{4,36},{5,37},{6,38},{7,39},{8,40},{9,... | collective-permute-start | bytes 786440 | tf_op jit(solution)/shard_map/ppermute | solution.py:44
  66.0 12.9 %collective-permute-start.13 = (bf16[1,4,4,64,128]{4,3,2,1,0:T(8,128)(2,1)S(1)}, bf16[1,4,4,64,128]{4,3,2,1,0:T(8,128)(2,1)S(1)}, u32[]{:S(2)}, u32[]{:S(2)}) collective-permute-start(bf16[1,4,4,64,128]{4,3,2,1,0:T(8,128)(2,1)S(1)} %get-tuple-element.65), channel_id=1, source_target_pairs={{0,32},{1,33},{2,34},{3,35},{4,36},{5,37},{6,38},{7,39},{8,40},{9,... | collective-permute-start | bytes 786440 | tf_op jit(solution)/shard_map/ppermute | solution.py:44
  67.2 23.6 %collective-permute-start.7 = (bf16[2,4,2,64,128]{4,3,2,1,0:T(8,128)(2,1)S(1)}, bf16[2,4,2,64,128]{4,3,2,1,0:T(8,128)(2,1)S(1)}, u32[]{:S(2)}, u32[]{:S(2)}) collective-permute-start(bf16[2,4,2,64,128]{4,3,2,1,0:T(8,128)(2,1)S(1)} %get-tuple-element.58), channel_id=1, source_target_pairs={{0,2},{1,3},{2,0},{3,1},{4,6},{5,7},{6,4},{7,5},{8,40},{9,41},{10,... | collective-permute-start | bytes 786440 | tf_op jit(solution)/shard_map/ppermute | solution.py:44
  73.2 18.8 %collective-permute-start.8 = (bf16[2,4,2,64,128]{4,3,2,1,0:T(8,128)(2,1)S(1)}, bf16[2,4,2,64,128]{4,3,2,1,0:T(8,128)(2,1)S(1)}, u32[]{:S(2)}, u32[]{:S(2)}) collective-permute-start(bf16[2,4,2,64,128]{4,3,2,1,0:T(8,128)(2,1)S(1)} %get-tuple-element.59), channel_id=1, source_target_pairs={{0,1},{1,2},{2,3},{3,0},{4,5},{5,6},{6,7},{7,4},{8,24},{9,25},{10,... | collective-permute-start | bytes 786440 | tf_op jit(solution)/shard_map/ppermute | solution.py:44
  78.9 13.0 %collective-permute-start.9 = (bf16[2,4,2,64,128]{4,3,2,1,0:T(8,128)(2,1)S(1)}, bf16[2,4,2,64,128]{4,3,2,1,0:T(8,128)(2,1)S(1)}, u32[]{:S(2)}, u32[]{:S(2)}) collective-permute-start(bf16[2,4,2,64,128]{4,3,2,1,0:T(8,128)(2,1)S(1)} %get-tuple-element.60), channel_id=1, source_target_pairs={{0,3},{1,0},{2,1},{3,2},{4,7},{5,4},{6,5},{7,6},{8,56},{9,57},{10,... | collective-permute-start | bytes 786440 | tf_op jit(solution)/shard_map/ppermute | solution.py:44
  87.5 9.8 %collective-permute-start.17 = (bf16[2,4,64,128]{3,2,1,0:T(8,128)(2,1)S(1)}, bf16[2,4,64,128]{3,2,1,0:T(8,128)(2,1)S(1)}, u32[]{:S(2)}, u32[]{:S(2)}) collective-permute-start(bf16[2,4,64,128]{3,2,1,0:T(8,128)(2,1)S(1)} %get-tuple-element.71), channel_id=1, source_target_pairs={{0,64},{1,65},{2,66},{3,67},{4,68},{5,69},{6,70},{7,71},{8,72},{9,... | collective-permute-start | bytes 393224 | tf_op jit(solution)/shard_map/ppermute | solution.py:44
  88.7 9.1 %collective-permute-start.18 = (bf16[2,4,64,128]{3,2,1,0:T(8,128)(2,1)S(1)}, bf16[2,4,64,128]{3,2,1,0:T(8,128)(2,1)S(1)}, u32[]{:S(2)}, u32[]{:S(2)}) collective-permute-start(bf16[2,4,64,128]{3,2,1,0:T(8,128)(2,1)S(1)} %get-tuple-element.72), channel_id=1, source_target_pairs={{0,4},{1,5},{2,6},{3,7},{4,64},{5,65},{6,66},{7,67},{8,12},{9,13},... | collective-permute-start | bytes 393224 | tf_op jit(solution)/shard_map/ppermute | solution.py:44
  90.8 7.0 %collective-permute-start.19 = (bf16[2,4,64,128]{3,2,1,0:T(8,128)(2,1)S(1)}, bf16[2,4,64,128]{3,2,1,0:T(8,128)(2,1)S(1)}, u32[]{:S(2)}, u32[]{:S(2)}) collective-permute-start(bf16[2,4,64,128]{3,2,1,0:T(8,128)(2,1)S(1)} %get-tuple-element.73), channel_id=1, source_target_pairs={{0,68},{1,69},{2,70},{3,71},{4,0},{5,1},{6,2},{7,3},{8,76},{9,77},... | collective-permute-start | bytes 393224 | tf_op jit(solution)/shard_map/ppermute | solution.py:44
  92.6 5.8 %collective-permute-start.14 = (bf16[2,2,64,128]{3,2,1,0:T(8,128)(2,1)S(1)}, bf16[2,2,64,128]{3,2,1,0:T(8,128)(2,1)S(1)}, u32[]{:S(2)}, u32[]{:S(2)}) collective-permute-start(bf16[2,2,64,128]{3,2,1,0:T(8,128)(2,1)S(1)} %get-tuple-element.68), channel_id=1, source_target_pairs={{0,32},{1,33},{2,34},{3,35},{4,36},{5,37},{6,38},{7,39},{8,72},{9,... | collective-permute-start | bytes 196616 | tf_op jit(solution)/shard_map/ppermute | solution.py:44
  92.7 6.5 %collective-permute-start.15 = (bf16[2,2,64,128]{3,2,1,0:T(8,128)(2,1)S(1)}, bf16[2,2,64,128]{3,2,1,0:T(8,128)(2,1)S(1)}, u32[]{:S(2)}, u32[]{:S(2)}) collective-permute-start(bf16[2,2,64,128]{3,2,1,0:T(8,128)(2,1)S(1)} %get-tuple-element.69), channel_id=1, source_target_pairs={{0,16},{1,17},{2,18},{3,19},{4,20},{5,21},{6,22},{7,23},{8,12},{9,... | collective-permute-start | bytes 196616 | tf_op jit(solution)/shard_map/ppermute | solution.py:44
  97.3 4.3 %collective-permute-start.16 = (bf16[2,2,64,128]{3,2,1,0:T(8,128)(2,1)S(1)}, bf16[2,2,64,128]{3,2,1,0:T(8,128)(2,1)S(1)}, u32[]{:S(2)}, u32[]{:S(2)}) collective-permute-start(bf16[2,2,64,128]{3,2,1,0:T(8,128)(2,1)S(1)} %get-tuple-element.70), channel_id=1, source_target_pairs={{0,48},{1,49},{2,50},{3,51},{4,52},{5,53},{6,54},{7,55},{8,76},{9,... | collective-permute-start | bytes 196616 | tf_op jit(solution)/shard_map/ppermute | solution.py:44
  102.1 8.7 %collective-permute-start.20 = (f32[2,64,128]{2,1,0:T(8,128)S(1)}, f32[2,64,128]{2,1,0:T(8,128)S(1)}, u32[]{:S(2)}, u32[]{:S(2)}) collective-permute-start(f32[2,64,128]{2,1,0:T(8,128)S(1)} %get-tuple-element.76), channel_id=1, source_target_pairs={{0,8},{1,9},{2,10},{3,11},{4,12},{5,13},{6,14},{7,15},{8,0},{9,1},... | collective-permute-start | bytes 196616 | tf_op jit(solution)/shard_map/ppermute | solution.py:52
  102.2 5.5 %collective-permute-start.21 = (bf16[2,64,128]{2,1,0:T(8,128)(2,1)S(1)}, bf16[2,64,128]{2,1,0:T(8,128)(2,1)S(1)}, u32[]{:S(2)}, u32[]{:S(2)}) collective-permute-start(bf16[2,64,128]{2,1,0:T(8,128)(2,1)S(1)} %get-tuple-element.77), channel_id=1, source_target_pairs={{0,2},{1,3},{2,0},{3,1},{4,6},{5,7},{6,4},{7,5},{8,10},{9,11},{10,... | collective-permute-start | bytes 98312 | tf_op jit(solution)/shard_map/ppermute | solution.py:44
  103.5 4.2 %collective-permute-start.22 = (bf16[2,64,128]{2,1,0:T(8,128)(2,1)S(1)}, bf16[2,64,128]{2,1,0:T(8,128)(2,1)S(1)}, u32[]{:S(2)}, u32[]{:S(2)}) collective-permute-start(bf16[2,64,128]{2,1,0:T(8,128)(2,1)S(1)} %get-tuple-element.78), channel_id=1, source_target_pairs={{0,1},{1,2},{2,3},{3,0},{4,5},{5,6},{6,7},{7,4},{8,9},{9,10},{10,1... | collective-permute-start | bytes 98312 | tf_op jit(solution)/shard_map/ppermute | solution.py:44
  105.7 5.1 %collective-permute-start.23 = (bf16[2,64,128]{2,1,0:T(8,128)(2,1)S(1)}, bf16[2,64,128]{2,1,0:T(8,128)(2,1)S(1)}, u32[]{:S(2)}, u32[]{:S(2)}) collective-permute-start(bf16[2,64,128]{2,1,0:T(8,128)(2,1)S(1)} %get-tuple-element.79), channel_id=1, source_target_pairs={{0,3},{1,0},{2,1},{3,2},{4,7},{5,4},{6,5},{7,6},{8,11},{9,8},{10,9... | collective-permute-start | bytes 98312 | tf_op jit(solution)/shard_map/ppermute | solution.py:44

commit v2 on v1

--- a/solution.py
+++ b/solution.py
@@ -65,7 +65,8 @@
 ANY = pl.BlockSpec(memory_space=pl.ANY)
 LIM = 12
 CHUNK = 2 * COLORS * LANES
-CHUNKS = WIDTH // CHUNK
+SPAN = 2 * CHUNK
+SPANS = WIDTH // SPAN
 
 
 def pack_columns(meta, step, block_ref, peer_ref):
@@ -82,48 +83,71 @@
     peer_ref[:, pl.ds(target, LANES)] = block_ref[:, pl.ds(source, LANES)]
 
 
-def preact_kernel(meta, tok_ref, w_ref, out_ref, peer_ref):
+def span(step):
+    return pl.ds(pl.multiple_of(step * SPAN, SPAN), SPAN)
+
+
+def copies(rows_ref, w_ref, w_axis, rows_buf, w_buf, sems):
+    def pair(step):
+        w_at = (span(step), slice(None)) if w_axis == 0 else (slice(None), span(step))
+        return (
+            pltpu.make_async_copy(rows_ref.at[:, span(step)], rows_buf.at[:, span(step)], sems.at[0, step]),
+            pltpu.make_async_copy(w_ref.at[*w_at], w_buf.at[*w_at], sems.at[1, step]),
+        )
+
+    return pair
+
+
+def preact_kernel(meta, tok_ref, w_ref, out_ref, peer_ref, tok_buf, w_buf, sems):
+    pair = copies(tok_ref, w_ref, 0, tok_buf, w_buf, sems)
+    for step in range(SPANS):
+        for copy in pair(step):
+            copy.start()
     out_ref[...] = jnp.zeros_like(out_ref)
 
-    def body(pair, _):
-        at = pl.ds(pl.multiple_of(pair * 2 * CHUNK, 2 * CHUNK), 2 * CHUNK)
-        out_ref[...] += jnp.dot(tok_ref[:, at], w_ref[at, :], preferred_element_type=F32)
+    def body(step, _):
+        for copy in pair(step):
+            copy.wait()
+        out_ref[...] += jnp.dot(tok_buf[:, span(step)], w_buf[span(step), :], preferred_element_type=F32)
         for half in range(2):
-            pack_columns(meta, pair * 2 + half, tok_ref, peer_ref)
+            pack_columns(meta, step * 2 + half, tok_buf, peer_ref)
         return 0
 
-    lax.fori_loop(0, CHUNKS // 2, body, 0)
-
-
-def hidden_kernel(meta, grad_ref, w_ref, preact_ref, hid_ref, peer_ref, acc_ref, slope_ref):
+    lax.fori_loop(0, SPANS, body, 0)
+
+
+def hidden_kernel(
+    meta, grad_ref, w_ref, preact_ref, hid_ref, peer_ref, acc_ref, slope_ref, grad_buf, w_buf, sems
+):
+    pair = copies(grad_ref, w_ref, 1, grad_buf, w_buf, sems)
+    for step in range(SPANS):
+        for copy in pair(step):
+            copy.start()
     acc_ref[...] = jnp.zeros_like(acc_ref)
 
-    def body(pair, _):
-        rows = pl.ds(pl.multiple_of(pair * LANES, LANES), LANES)
+    def body(step, _):
+        for copy in pair(step):
+            copy.wait()
+        rows = pl.ds(pl.multiple_of(step * LANES, LANES), LANES)
         preact = preact_ref[rows, :].T
         cumul = 0.5 * (1.0 + lax.erf(preact * (1.0 / math.sqrt(2.0))))
         density = jnp.exp(-0.5 * preact * preact) * (1.0 / math.sqrt(2.0 * math.pi))
         hid_ref[:, rows] = (preact * cumul).astype(BF16)
         slope_ref[:, rows] = cumul + preact * density
-        at = pl.ds(pl.multiple_of(pair * 2 * CHUNK, 2 * CHUNK), 2 * CHUNK)
         acc_ref[...] += lax.dot_general(
-            w_ref[:, at], grad_ref[:, at], (((1,), (1,)), ((), ())), preferred_element_type=F32
+            w_buf[:, span(step)], grad_buf[:, span(step)], (((1,), (1,)), ((), ())), preferred_element_type=F32
         )
         for half in range(2):
-            pack_columns(meta, pair * 2 + half, grad_ref, peer_ref)
+            pack_columns(meta, step * 2 + half, grad_buf, peer_ref)
         return 0
 
-    lax.fori_loop(0, CHUNKS // 2, body, 0)
+    lax.fori_loop(0, SPANS, body, 0)
     hid_ref[:, TOK : 2 * TOK] = (acc_ref[...] * slope_ref[...]).astype(BF16)
 
 
-def term_kernel(meta, *refs, which, first):
+def term_kernel(meta, *refs, which):
     hid, hid_peer, full, peer = refs[:4]
-    refs = refs[4 + (0 if first else 6) :]
-    out_at = {0: (0, which), 1: (1, which), 3: (2, which), 2: (6, 0)}
-    major = {d: refs[i].at[t] for d, (i, t) in out_at.items()}
-    minor = {d: refs[i + (3 if d != 2 else 1)].at[t] for d, (i, t) in out_at.items()}
-    scr = refs[8]
+    major, minor, scr = refs[4:8], refs[8:12], refs[12]
     core, own_x, own_y, own_z = meta[0], meta[1], meta[2], meta[3]
     lhs = slice((which == 1) * TOK, (which == 1) * TOK + TOK)
 
@@ -179,22 +203,16 @@
     return jax.ShapeDtypeStruct(dims, BF16)
 
 
-def term_call(meta, which, hid, hid_peer, full, peer, buffers):
-    operands = [meta, hid, hid_peer, full, peer]
-    aliases = {}
-    if buffers is not None:
-        aliases = {len(operands) + i: i for i in range(6)}
-        operands += list(buffers)
+def term_call(meta, which, hid, hid_peer, full, peer):
     return pl.pallas_call(
-        functools.partial(term_kernel, which=which, first=buffers is None),
-        in_specs=[SMEM] + [VMEM] * (len(operands) - 1),
+        functools.partial(term_kernel, which=which),
+        in_specs=[SMEM] + [VMEM] * 4,
         out_specs=[VMEM] * 8,
-        out_shape=[bf16(2, *MAJOR1)] * 3 + [bf16(2, *MINOR1)] * 3 + [bf16(1, *MAJOR1), bf16(1, *MINOR1)],
+        out_shape=[bf16(*MAJOR1)] * 4 + [bf16(*MINOR1)] * 4,
         scratch_shapes=[pltpu.VMEM((2, 4, HID, LANES), BF16)],
-        input_output_aliases=aliases,
         compiler_params=limit(LIM),
         cost_estimate=cost(4 * TOK * HID * HALF, 12 * 1024 * 1024),
-    )(*operands)
+    )(meta, hid, hid_peer, full, peer)
 
 
 def total(pieces):
@@ -206,7 +224,7 @@
 
 def major1_kernel(meta, *refs):
     core = meta[0]
-    parts, two, out = refs[:3], refs[3:5], refs[5:9]
+    terms, out = (refs[0:4], refs[4:8]), refs[8:12]
     for e in range(4):
 
         def body(f, _):
@@ -214,21 +232,19 @@
             w = jnp.where(core == 0, e, f)
             for t in range(2):
                 for cp in range(2):
-                    pieces = [part[t, j, cp, w] for part in parts] + [two[t][0, j, cp, w]]
-                    out[e][t, f, cp] = total(pieces).astype(BF16)
+                    out[e][t, f, cp] = total([part[j, cp, w] for part in terms[t]]).astype(BF16)
             return 0
 
         lax.fori_loop(0, 4, body, 0)
 
 
 def minor1_kernel(meta, *refs):
-    parts, two, out = refs[:3], refs[3:5], refs[6:10]
+    terms, out = (refs[0:4], refs[4:8]), refs[9:13]
     for e in range(4):
 
         def body(f, _):
             for t in range(2):
-                pieces = [part[t, e, f] for part in parts] + [two[t][0, e, f]]
-                out[e][t, f] = total(pieces).astype(BF16)
+                out[e][t, f] = total([part[e, f] for part in terms[t]]).astype(BF16)
             return 0
 
         lax.fori_loop(0, 4, body, 0)
@@ -272,16 +288,15 @@
         in_specs.append(ANY)
         operands.append(after)
     return pl.pallas_call(
-        kernel,
-        in_specs=in_specs,
-        out_specs=[VMEM] * len(shapes),
-        out_shape=shapes,
-        compiler_params=limit(LIM),
+        kernel, in_specs=in_specs, out_specs=[VMEM] * len(shapes), out_shape=shapes, compiler_params=limit(LIM)
     )(*operands)
 
 
 def ring(parts, axis0, axis1):
-    return [parts[0]] + [shift(parts[d], axis0, axis1, d) for d in (2, 1, 3)]
+    got = [parts[0]]
+    for d in (2, 1, 3):
+        got.append(shift(parts[d], axis0, axis1, d))
+    return got
 
 
 def local(tokens, grad_out, w_up, w_down):
@@ -294,10 +309,15 @@
 
     preact, pack_tok = pl.pallas_call(
         preact_kernel,
-        in_specs=[SMEM, VMEM, VMEM],
+        in_specs=[SMEM, ANY, ANY],
         out_specs=[VMEM] * 2,
         out_shape=[jax.ShapeDtypeStruct((TOK, HID), F32), bf16(TOK, HALF)],
-        compiler_params=limit(LIM),
+        scratch_shapes=[
+            pltpu.VMEM((TOK, WIDTH), BF16),
+            pltpu.VMEM((WIDTH, HID), BF16),
+            pltpu.SemaphoreType.DMA((2, SPANS)),
+        ],
+        compiler_params=limit(50),
         cost_estimate=cost(2 * TOK * HID * WIDTH, 16 * 1024 * 1024),
         name="preact",
     )(meta, tokens, w_up)
@@ -305,39 +325,37 @@
 
     hid, pack_grad = pl.pallas_call(
         hidden_kernel,
-        in_specs=[SMEM, VMEM, VMEM, VMEM],
+        in_specs=[SMEM, ANY, ANY, VMEM],
         out_specs=[VMEM] * 2,
         out_shape=[bf16(HID, 2 * TOK), bf16(TOK, HALF)],
-        scratch_shapes=[pltpu.VMEM((HID, TOK), F32), pltpu.VMEM((HID, TOK), F32)],
-        compiler_params=limit(LIM),
+        scratch_shapes=[
+            pltpu.VMEM((HID, TOK), F32),
+            pltpu.VMEM((HID, TOK), F32),
+            pltpu.VMEM((TOK, WIDTH), BF16),
+            pltpu.VMEM((HID, WIDTH), BF16),
+            pltpu.SemaphoreType.DMA((2, SPANS)),
+        ],
+        compiler_params=limit(44),
         cost_estimate=cost(2 * TOK * HID * WIDTH, 18 * 1024 * 1024),
         name="hidden",
     )(meta, grad_out, w_down, preact)
     hid_peer = swap(hid)
     peer_grad = swap(pack_grad)
 
-    out = term_call(meta, 1, hid, hid_peer, tokens, peer_tok, None)
-    major_up = shift(out[6], "x", "y", 2)
-    minor_up = shift(out[7], "z", "z", 2)
-    out = term_call(meta, 0, hid, hid_peer, grad_out, peer_grad, out[:6])
-
-    major_two = [shift(out[6], "x", "y", 2), major_up]
-    minor_two = [shift(out[7], "z", "z", 2), minor_up]
-    major = [out[0], shift(out[1], "x", "y", 1), shift(out[2], "x", "y", 3)]
-    minor = [out[3], shift(out[4], "z", "z", 1), shift(out[5], "z", "z", 3)]
-    major = sum_call(major1_kernel, meta, major + major_two, [bf16(2, 4, 2, SUB, LANES)] * 4)
-    minor = sum_call(minor1_kernel, meta, minor + minor_two, [bf16(2, 4, SUB, LANES)] * 4, major[0])
-    major = ring(major, "y", "z")
-    last = minor[0]
+    up = term_call(meta, 1, hid, hid_peer, tokens, peer_tok)
+    down = term_call(meta, 0, hid, hid_peer, grad_out, peer_grad)
+    up_major, up_minor = ring(up[:4], "x", "y"), ring(up[4:], "z", "z")
+    major, minor = ring(down[:4], "x", "y"), ring(down[4:], "z", "z")
+
+    major = sum_call(major1_kernel, meta, major + up_major, [bf16(2, 4, 2, SUB, LANES)] * 4)
+    minor = sum_call(minor1_kernel, meta, minor + up_minor, [bf16(2, 4, SUB, LANES)] * 4, major[0])
+    major, last = ring(major, "y", "z"), minor[0]
     minor = ring(minor, "x", "x")
     major = sum_call(major2_kernel, meta, major, [bf16(2, 2, SUB, LANES)] * 4, last)
     minor = sum_call(minor2_kernel, meta, minor, [bf16(2, SUB, LANES)] * 4, major[0])
-    major = ring(major, "z", "x")
-    last = minor[0]
+    major, last = ring(major, "z", "x"), minor[0]
     minor = ring(minor, "y", "y")
-    keep, send = sum_call(
-        major3_kernel, meta, major, [jax.ShapeDtypeStruct((2, SUB, LANES), F32)] * 2, last
-    )
+    keep, send = sum_call(major3_kernel, meta, major, [jax.ShapeDtypeStruct((2, SUB, LANES), F32)] * 2, last)
     total_tokens = tokens.shape[0] * lax.axis_size("row") * lax.axis_size("col")
     up, down = sum_call(
         functools.partial(final_kernel, factor=1.0 / math.sqrt(total_tokens)),

time: 112 us -> 102 us (0.911)
  the two profiles are of different devices: /device:TPU:24 before, /device:TPU:26 now
where the time goes in v2:
time: 102 us
  starting transfers between devices  42.9 us (42%)
  Pallas kernels  29.9 us (29%)
  waiting for transfers between devices  28 us (27%)
    ppermute x24, starting transfers between devices, shift(): return lax.ppermute(value, AXES, pairs)  42.2 us
    ppermute x24, waiting for transfers between devices, shift(): return lax.ppermute(value, AXES, pairs)  17 us
    ppermute x4, waiting for transfers between devices, swap(): return lax.ppermute(value, AXES, pairs)  11.1 us
    pallas_call x2, Pallas kernels, term_call(): pl.pallas_call(functools.partial(term_kernel, which=which), in_specs=[SME...  8.8 us
    pallas_call x1, Pallas kernels, local(): pl.pallas_call(preact_kernel, in_specs=[SMEM, ANY, ANY], out_specs=[VMEM]...  8.07 us
    pallas_call x1, Pallas kernels, local(): pl.pallas_call(hidden_kernel, in_specs=[SMEM, ANY, ANY, VMEM], out_specs=...  7.85 us
    pallas_call x6, Pallas kernels, sum_call(): pl.pallas_call(kernel, in_specs=in_specs, out_specs=[VMEM] * len(shapes),...  5.16 us
  transfers between devices with their start and end apart: 28, of which 8 were waited for; matrix products, arithmetic and copies ran while one was open for 0% of the time, Pallas kernels for 12%

profile of v2, /device:TPU:26, one launch (start us, length us, event | category | flops | bytes accessed | tf_op | source)
XLA Modules:
  0.0 101.8 jit_solution(4197708063707908052)
XLA Ops:
  0.7 0.0 slice-start
  0.7 8.1 %preact.1 = (f32[512,512]{1,0:T(8,128)S(1)}, bf16[512,3072]{1,0:T(8,128)(2,1)}) custom-call(s32[4]{0:T(128)S(1)} %compare_select_fusion.2.meta, bf16[512,6144]{1,0:T(8,128)(2,1)} %refs_2_.3, bf16[6144,512]{1,0:T(8,128)(2,1)} %w_ref.2), custom_call_target="tpu_custom_call" | custom-call | flops 3221225472 | bytes 16777216 | tf_op jit(solution)/shard_map/preact/pallas_call | solution.py:310
  8.8 0.0 slice-start.1
  8.8 7.8 %hidden.1 = (bf16[512,1024]{1,0:T(8,128)(2,1)S(1)}, bf16[512,3072]{1,0:T(8,128)(2,1)S(1)}) custom-call(s32[4]{0:T(128)S(1)} %compare_select_fusion.2.meta, bf16[512,6144]{1,0:T(8,128)(2,1)} %refs_2_.2, bf16[512,6144]{1,0:T(8,128)(2,1)} %w_ref.3, f32[512,512]{1,0:T(8,128)S(1)} %get-tuple-element.42.preact_ref), custom_call_target="tpu_custom_call" | custom-call | flops 3221225472 | bytes 18874368 | tf_op jit(solution)/shard_map/hidden/pallas_call | solution.py:326
  16.7 0.0 slice-start.2
  16.7 0.1 collective-permute-start.1
  16.8 0.5 collective-permute-start.5
  17.3 0.1 collective-permute-start
  17.4 11.0 %collective-permute-done.refs_1_ = bf16[512,1024]{1,0:T(8,128)(2,1)S(1)} collective-permute-done((bf16[512,1024]{1,0:T(8,128)(2,1)S(1)}, bf16[512,1024]{1,0:T(8,128)(2,1)S(1)}, u32[]{:S(2)}, u32[]{:S(2)}) %collective-permute-start) | collective-permute-done | bytes 1048608 | tf_op jit(solution)/shard_map/ppermute | solution.py:52
  28.5 0.0 collective-permute-done.1.refs_3_
  28.5 4.4 %shard_map.59 = (bf16[4,2,4,64,128]{4,3,2,1,0:T(8,128)(2,1)S(1)}, bf16[4,2,4,64,128]{4,3,2,1,0:T(8,128)(2,1)S(1)}, bf16[4,2,4,64,128]{4,3,2,1,0:T(8,128)(2,1)S(1...) custom-call(s32[4]{0:T(128)S(1)} %compare_select_fusion.2.meta, ...), custom_call_target="tpu_custom_call" | custom-call | flops 3221225472 | bytes 12582912 | tf_op jit(solution)/shard_map/pallas_call | solution.py:207
  32.9 2.2 %collective-permute-start.2 = (bf16[4,2,4,64,128]{4,3,2,1,0:T(8,128)(2,1)S(1)}, bf16[4,2,4,64,128]{4,3,2,1,0:T(8,128)(2,1)S(1)}, u32[]{:S(2)}, u32[]{:S(2)}) collective-permute-start(bf16[4,2,4,64,128]{4,3,2,1,0:T(8,128)(2,1)S(1)} %get-tuple-element.46), channel_id=1, source_target_pairs={{0,64},{1,65},{2,66},{3,67},{4,68},{5,69},{6,70},{7,71},{8,10},{9,... | collective-permute-start | bytes 1572872 | tf_op jit(solution)/shard_map/ppermute | solution.py:44
  35.1 3.9 %collective-permute-start.12 = (bf16[4,4,64,128]{3,2,1,0:T(8,128)(2,1)S(1)}, bf16[4,4,64,128]{3,2,1,0:T(8,128)(2,1)S(1)}, u32[]{:S(2)}, u32[]{:S(2)}) collective-permute-start(bf16[4,4,64,128]{3,2,1,0:T(8,128)(2,1)S(1)} %get-tuple-element.59), channel_id=1, source_target_pairs={{0,32},{1,33},{2,34},{3,35},{4,36},{5,37},{6,38},{7,39},{8,40},{9,... | collective-permute-start | bytes 786440 | tf_op jit(solution)/shard_map/ppermute | solution.py:44
  38.9 0.0 collective-permute-start.3
  38.9 2.0 %collective-permute-start.4 = (bf16[4,2,4,64,128]{4,3,2,1,0:T(8,128)(2,1)S(1)}, bf16[4,2,4,64,128]{4,3,2,1,0:T(8,128)(2,1)S(1)}, u32[]{:S(2)}, u32[]{:S(2)}) collective-permute-start(bf16[4,2,4,64,128]{4,3,2,1,0:T(8,128)(2,1)S(1)} %get-tuple-element.48), channel_id=1, source_target_pairs={{0,68},{1,69},{2,70},{3,71},{4,0},{5,1},{6,2},{7,3},{8,11},{9,8},{... | collective-permute-start | bytes 1572872 | tf_op jit(solution)/shard_map/ppermute | solution.py:44
  41.0 0.0 collective-permute-done.5.refs_3_
  41.0 4.4 %shard_map.60 = (bf16[4,2,4,64,128]{4,3,2,1,0:T(8,128)(2,1)S(1)}, bf16[4,2,4,64,128]{4,3,2,1,0:T(8,128)(2,1)S(1)}, bf16[4,2,4,64,128]{4,3,2,1,0:T(8,128)(2,1)S(1...) custom-call(s32[4]{0:T(128)S(1)} %compare_select_fusion.2.meta, ...), custom_call_target="tpu_custom_call" | custom-call | flops 3221225472 | bytes 12582912 | tf_op jit(solution)/shard_map/pallas_call | solution.py:207
  45.4 1.6 %collective-permute-start.6 = (bf16[4,2,4,64,128]{4,3,2,1,0:T(8,128)(2,1)S(1)}, bf16[4,2,4,64,128]{4,3,2,1,0:T(8,128)(2,1)S(1)}, u32[]{:S(2)}, u32[]{:S(2)}) collective-permute-start(bf16[4,2,4,64,128]{4,3,2,1,0:T(8,128)(2,1)S(1)} %get-tuple-element.51), channel_id=1, source_target_pairs={{0,64},{1,65},{2,66},{3,67},{4,68},{5,69},{6,70},{7,71},{8,10},{9,... | collective-permute-start | bytes 1572872 | tf_op jit(solution)/shard_map/ppermute | solution.py:44
  47.0 2.6 %collective-permute-start.7 = (bf16[4,2,4,64,128]{4,3,2,1,0:T(8,128)(2,1)S(1)}, bf16[4,2,4,64,128]{4,3,2,1,0:T(8,128)(2,1)S(1)}, u32[]{:S(2)}, u32[]{:S(2)}) collective-permute-start(bf16[4,2,4,64,128]{4,3,2,1,0:T(8,128)(2,1)S(1)} %get-tuple-element.52), channel_id=1, source_target_pairs={{0,4},{1,5},{2,6},{3,7},{4,64},{5,65},{6,66},{7,67},{8,9},{9,10},{... | collective-permute-start | bytes 1572872 | tf_op jit(solution)/shard_map/ppermute | solution.py:44
  49.6 1.6 %collective-permute-start.13 = (bf16[4,4,64,128]{3,2,1,0:T(8,128)(2,1)S(1)}, bf16[4,4,64,128]{3,2,1,0:T(8,128)(2,1)S(1)}, u32[]{:S(2)}, u32[]{:S(2)}) collective-permute-start(bf16[4,4,64,128]{3,2,1,0:T(8,128)(2,1)S(1)} %get-tuple-element.60), channel_id=1, source_target_pairs={{0,16},{1,17},{2,18},{3,19},{4,20},{5,21},{6,22},{7,23},{8,24},{9,... | collective-permute-start | bytes 786440 | tf_op jit(solution)/shard_map/ppermute | solution.py:44
  51.2 2.1 %collective-permute-start.14 = (bf16[4,4,64,128]{3,2,1,0:T(8,128)(2,1)S(1)}, bf16[4,4,64,128]{3,2,1,0:T(8,128)(2,1)S(1)}, u32[]{:S(2)}, u32[]{:S(2)}) collective-permute-start(bf16[4,4,64,128]{3,2,1,0:T(8,128)(2,1)S(1)} %get-tuple-element.61), channel_id=1, source_target_pairs={{0,48},{1,49},{2,50},{3,51},{4,52},{5,53},{6,54},{7,55},{8,56},{9,... | collective-permute-start | bytes 786440 | tf_op jit(solution)/shard_map/ppermute | solution.py:44
  53.4 2.9 %collective-permute-done.6.refs_5_ = bf16[4,2,4,64,128]{4,3,2,1,0:T(8,128)(2,1)S(1)} collective-permute-done((bf16[4,2,4,64,128]{4,3,2,1,0:T(8,128)(2,1)S(1)}, bf16[4,2,4,64,128]{4,3,2,1,0:T(8,128)(2,1)S(1)}, u32[]{:S(2)}, u32[]{:S(2)}) %collective-permute-start.6) | collective-permute-done | bytes 524320 | tf_op jit(solution)/shard_map/ppermute | solution.py:44
  56.3 2.6 %collective-permute-start.15 = (bf16[4,4,64,128]{3,2,1,0:T(8,128)(2,1)S(1)}, bf16[4,4,64,128]{3,2,1,0:T(8,128)(2,1)S(1)}, u32[]{:S(2)}, u32[]{:S(2)}) collective-permute-start(bf16[4,4,64,128]{3,2,1,0:T(8,128)(2,1)S(1)} %get-tuple-element.63), channel_id=1, source_target_pairs={{0,32},{1,33},{2,34},{3,35},{4,36},{5,37},{6,38},{7,39},{8,40},{9,... | collective-permute-start | bytes 786440 | tf_op jit(solution)/shard_map/ppermute | solution.py:44
  58.9 2.1 %collective-permute-done.7.refs_6_ = bf16[4,2,4,64,128]{4,3,2,1,0:T(8,128)(2,1)S(1)} collective-permute-done((bf16[4,2,4,64,128]{4,3,2,1,0:T(8,128)(2,1)S(1)}, bf16[4,2,4,64,128]{4,3,2,1,0:T(8,128)(2,1)S(1)}, u32[]{:S(2)}, u32[]{:S(2)}) %collective-permute-start.7) | collective-permute-done | bytes 524320 | tf_op jit(solution)/shard_map/ppermute | solution.py:44
  61.0 1.6 %collective-permute-start.16 = (bf16[4,4,64,128]{3,2,1,0:T(8,128)(2,1)S(1)}, bf16[4,4,64,128]{3,2,1,0:T(8,128)(2,1)S(1)}, u32[]{:S(2)}, u32[]{:S(2)}) collective-permute-start(bf16[4,4,64,128]{3,2,1,0:T(8,128)(2,1)S(1)} %get-tuple-element.64), channel_id=1, source_target_pairs={{0,16},{1,17},{2,18},{3,19},{4,20},{5,21},{6,22},{7,23},{8,24},{9,... | collective-permute-start | bytes 786440 | tf_op jit(solution)/shard_map/ppermute | solution.py:44
  62.5 2.1 %collective-permute-start.17 = (bf16[4,4,64,128]{3,2,1,0:T(8,128)(2,1)S(1)}, bf16[4,4,64,128]{3,2,1,0:T(8,128)(2,1)S(1)}, u32[]{:S(2)}, u32[]{:S(2)}) collective-permute-start(bf16[4,4,64,128]{3,2,1,0:T(8,128)(2,1)S(1)} %get-tuple-element.65), channel_id=1, source_target_pairs={{0,48},{1,49},{2,50},{3,51},{4,52},{5,53},{6,54},{7,55},{8,56},{9,... | collective-permute-start | bytes 786440 | tf_op jit(solution)/shard_map/ppermute | solution.py:44
  64.6 1.2 %shard_map.61 = (bf16[2,4,2,64,128]{4,3,2,1,0:T(8,128)(2,1)S(1)}, bf16[2,4,2,64,128]{4,3,2,1,0:T(8,128)(2,1)S(1)}, bf16[2,4,2,64,128]{4,3,2,1,0:T(8,128)(2,1)S(1)}, bf16[2,4,2,64,128]{4,3,2,1,0:T(8,128)(2,1)S(1)}) custom-call(s32[4]{0:T(128)S(1)} %compare_select_fusion.2.meta, bf16[4,2,4,64,128]{4,3,2,1,0:T(8,128)(2,1)S(1)} %get-tuple-element.45.refs_0_, ...), custom_call_target="tpu_custom_call" | custom-call | tf_op jit(solution)/shard_map/pallas_call | solution.py:290
  65.8 1.3 %collective-permute-start.9 = (bf16[2,4,2,64,128]{4,3,2,1,0:T(8,128)(2,1)S(1)}, bf16[2,4,2,64,128]{4,3,2,1,0:T(8,128)(2,1)S(1)}, u32[]{:S(2)}, u32[]{:S(2)}) collective-permute-start(bf16[2,4,2,64,128]{4,3,2,1,0:T(8,128)(2,1)S(1)} %get-tuple-element.55), channel_id=1, source_target_pairs={{0,2},{1,3},{2,0},{3,1},{4,6},{5,7},{6,4},{7,5},{8,40},{9,41},{10,... | collective-permute-start | bytes 786440 | tf_op jit(solution)/shard_map/ppermute | solution.py:44
  67.2 2.2 %collective-permute-start.10 = (bf16[2,4,2,64,128]{4,3,2,1,0:T(8,128)(2,1)S(1)}, bf16[2,4,2,64,128]{4,3,2,1,0:T(8,128)(2,1)S(1)}, u32[]{:S(2)}, u32[]{:S(2)}) collective-permute-start(bf16[2,4,2,64,128]{4,3,2,1,0:T(8,128)(2,1)S(1)} %get-tuple-element.56), channel_id=1, source_target_pairs={{0,1},{1,2},{2,3},{3,0},{4,5},{5,6},{6,7},{7,4},{8,24},{9,25},{10,... | collective-permute-start | bytes 786440 | tf_op jit(solution)/shard_map/ppermute | solution.py:44
  69.3 5.0 %collective-permute-done.16.refs_6_ = bf16[4,4,64,128]{3,2,1,0:T(8,128)(2,1)S(1)} collective-permute-done((bf16[4,4,64,128]{3,2,1,0:T(8,128)(2,1)S(1)}, bf16[4,4,64,128]{3,2,1,0:T(8,128)(2,1)S(1)}, u32[]{:S(2)}, u32[]{:S(2)}) %collective-permute-start.16) | collective-permute-done | bytes 262176 | tf_op jit(solution)/shard_map/ppermute | solution.py:44
  74.4 0.9 shard_map.62
  75.3 4.6 %collective-permute-start.21 = (bf16[2,4,64,128]{3,2,1,0:T(8,128)(2,1)S(1)}, bf16[2,4,64,128]{3,2,1,0:T(8,128)(2,1)S(1)}, u32[]{:S(2)}, u32[]{:S(2)}) collective-permute-start(bf16[2,4,64,128]{3,2,1,0:T(8,128)(2,1)S(1)} %get-tuple-element.71), channel_id=1, source_target_pairs={{0,64},{1,65},{2,66},{3,67},{4,68},{5,69},{6,70},{7,71},{8,72},{9,... | collective-permute-start | bytes 393224 | tf_op jit(solution)/shard_map/ppermute | solution.py:44
  79.8 0.3 collective-permute-start.22
  80.2 1.7 %collective-permute-start.23 = (bf16[2,4,64,128]{3,2,1,0:T(8,128)(2,1)S(1)}, bf16[2,4,64,128]{3,2,1,0:T(8,128)(2,1)S(1)}, u32[]{:S(2)}, u32[]{:S(2)}) collective-permute-start(bf16[2,4,64,128]{3,2,1,0:T(8,128)(2,1)S(1)} %get-tuple-element.73), channel_id=1, source_target_pairs={{0,68},{1,69},{2,70},{3,71},{4,0},{5,1},{6,2},{7,3},{8,76},{9,77},... | collective-permute-start | bytes 393224 | tf_op jit(solution)/shard_map/ppermute | solution.py:44
  81.9 0.7 shard_map.63
  82.6 3.0 %collective-permute-start.18 = (bf16[2,2,64,128]{3,2,1,0:T(8,128)(2,1)S(1)}, bf16[2,2,64,128]{3,2,1,0:T(8,128)(2,1)S(1)}, u32[]{:S(2)}, u32[]{:S(2)}) collective-permute-start(bf16[2,2,64,128]{3,2,1,0:T(8,128)(2,1)S(1)} %get-tuple-element.68), channel_id=1, source_target_pairs={{0,32},{1,33},{2,34},{3,35},{4,36},{5,37},{6,38},{7,39},{8,72},{9,... | collective-permute-start | bytes 196616 | tf_op jit(solution)/shard_map/ppermute | solution.py:44
  85.6 1.4 %collective-permute-start.19 = (bf16[2,2,64,128]{3,2,1,0:T(8,128)(2,1)S(1)}, bf16[2,2,64,128]{3,2,1,0:T(8,128)(2,1)S(1)}, u32[]{:S(2)}, u32[]{:S(2)}) collective-permute-start(bf16[2,2,64,128]{3,2,1,0:T(8,128)(2,1)S(1)} %get-tuple-element.69), channel_id=1, source_target_pairs={{0,16},{1,17},{2,18},{3,19},{4,20},{5,21},{6,22},{7,23},{8,12},{9,... | collective-permute-start | bytes 196616 | tf_op jit(solution)/shard_map/ppermute | solution.py:44
  87.0 1.9 %collective-permute-start.20 = (bf16[2,2,64,128]{3,2,1,0:T(8,128)(2,1)S(1)}, bf16[2,2,64,128]{3,2,1,0:T(8,128)(2,1)S(1)}, u32[]{:S(2)}, u32[]{:S(2)}) collective-permute-start(bf16[2,2,64,128]{3,2,1,0:T(8,128)(2,1)S(1)} %get-tuple-element.70), channel_id=1, source_target_pairs={{0,48},{1,49},{2,50},{3,51},{4,52},{5,53},{6,54},{7,55},{8,76},{9,... | collective-permute-start | bytes 196616 | tf_op jit(solution)/shard_map/ppermute | solution.py:44
  88.8 0.6 shard_map.64
  89.5 1.6 %collective-permute-done.19.refs_2_ = bf16[2,2,64,128]{3,2,1,0:T(8,128)(2,1)S(1)} collective-permute-done((bf16[2,2,64,128]{3,2,1,0:T(8,128)(2,1)S(1)}, bf16[2,2,64,128]{3,2,1,0:T(8,128)(2,1)S(1)}, u32[]{:S(2)}, u32[]{:S(2)}) %collective-permute-start.19) | collective-permute-done | bytes 65568 | tf_op jit(solution)/shard_map/ppermute | solution.py:44
  91.1 0.2 collective-permute-done.20.refs_3_
  91.2 0.6 shard_map.65
  91.8 0.1 collective-permute-start.24
  91.9 1.3 %collective-permute-start.25 = (bf16[2,64,128]{2,1,0:T(8,128)(2,1)S(1)}, bf16[2,64,128]{2,1,0:T(8,128)(2,1)S(1)}, u32[]{:S(2)}, u32[]{:S(2)}) collective-permute-start(bf16[2,64,128]{2,1,0:T(8,128)(2,1)S(1)} %get-tuple-element.77), channel_id=1, source_target_pairs={{0,2},{1,3},{2,0},{3,1},{4,6},{5,7},{6,4},{7,5},{8,10},{9,11},{10,... | collective-permute-start | bytes 98312 | tf_op jit(solution)/shard_map/ppermute | solution.py:44
  93.2 2.2 %collective-permute-start.26 = (bf16[2,64,128]{2,1,0:T(8,128)(2,1)S(1)}, bf16[2,64,128]{2,1,0:T(8,128)(2,1)S(1)}, u32[]{:S(2)}, u32[]{:S(2)}) collective-permute-start(bf16[2,64,128]{2,1,0:T(8,128)(2,1)S(1)} %get-tuple-element.78), channel_id=1, source_target_pairs={{0,1},{1,2},{2,3},{3,0},{4,5},{5,6},{6,7},{7,4},{8,9},{9,10},{10,1... | collective-permute-start | bytes 98312 | tf_op jit(solution)/shard_map/ppermute | solution.py:44
  95.4 2.0 %collective-permute-done.25.p1 = bf16[2,64,128]{2,1,0:T(8,128)(2,1)S(1)} collective-permute-done((bf16[2,64,128]{2,1,0:T(8,128)(2,1)S(1)}, bf16[2,64,128]{2,1,0:T(8,128)(2,1)S(1)}, u32[]{:S(2)}, u32[]{:S(2)}) %collective-permute-start.25) | collective-permute-done | bytes 32800 | tf_op jit(solution)/shard_map/ppermute | solution.py:44
  97.4 3.1 %collective-permute-done.27.p3 = bf16[2,64,128]{2,1,0:T(8,128)(2,1)S(1)} collective-permute-done((bf16[2,64,128]{2,1,0:T(8,128)(2,1)S(1)}, bf16[2,64,128]{2,1,0:T(8,128)(2,1)S(1)}, u32[]{:S(2)}, u32[]{:S(2)}) %collective-permute-start.27) | collective-permute-done | bytes 32800 | tf_op jit(solution)/shard_map/ppermute | solution.py:44
  100.5 1.2 %shard_map.66 = (f32[64,384]{1,0:T(8,128)}, f32[64,384]{1,0:T(8,128)}) custom-call(s32[4]{0:T(128)S(1)} %compare_select_fusion.2.meta, f32[2,64,128]{2,1,0:T(8,128)S(1)} %get-tuple-element.75.keep, f32[2,64,128]{2,1,0:T(8,128)S(1)} %collective-permute-done.24.got, bf16[2,64,128]{2,1,0:T(8,128)(2,1)S(1)} %get-tuple-element.74.refs_4_.p0, ...), custom_call_target="tpu_custom_call" | custom-call | tf_op jit(solution)/shard_map/pallas_call | solution.py:290
  (31 shorter events, 0.1 us)
Async XLA Ops:
  0.7 27.7 %slice-start = ((s8[6291456]{0:T(1024)(128)(4,1)}), s8[2097152]{0:T(1024)(128)(4,1)S(1)}, s32[]{:S(2)}) async-start(s8[6291456]{0:T(1024)(128)(4,1)} %bitcast.2), calls=%async_computation | async-start | bytes 4194304
  8.8 8.0 %copy-start = (bf16[512,3072]{1,0:T(8,128)(2,1)S(1)}, bf16[512,3072]{1,0:T(8,128)(2,1)}, u32[]{:S(2)}) copy-start(bf16[512,3072]{1,0:T(8,128)(2,1)} %get-tuple-element.49) | copy-start | bytes 9437188
  8.8 19.6 %slice-start.1 = ((s8[6291456]{0:T(1024)(128)(4,1)}), s8[4194304]{0:T(1024)(128)(4,1)S(1)}, s32[]{:S(2)}) async-start(s8[6291456]{0:T(1024)(128)(4,1)} %bitcast.2), calls=%async_computation.1 | async-start | bytes 8388608
  16.7 24.3 %slice-start.2 = ((s8[6291456]{0:T(1024)(128)(4,1)}), s8[4194304]{0:T(1024)(128)(4,1)S(1)}, s32[]{:S(2)}) async-start(s8[6291456]{0:T(1024)(128)(4,1)} %bitcast.4), calls=%async_computation.2 | async-start | bytes 8388608
  16.7 11.7 %collective-permute-start.1 = (bf16[512,3072]{1,0:T(8,128)(2,1)S(1)}, bf16[512,3072]{1,0:T(8,128)(2,1)S(1)}, u32[]{:S(2)}, u32[]{:S(2)}) collective-permute-start(bf16[512,3072]{1,0:T(8,128)(2,1)S(1)} %get-tuple-element.44), channel_id=1, source_target_pairs={{0,8},{1,9},{2,10},{3,11},{4,12},{5,13},{6,14},{7,15},{8,0},{9,1},... | collective-permute-start | bytes 9437192 | tf_op jit(solution)/shard_map/ppermute | solution.py:52
  16.8 24.1 %collective-permute-start.5 = (bf16[512,3072]{1,0:T(8,128)(2,1)S(1)}, bf16[512,3072]{1,0:T(8,128)(2,1)S(1)}, u32[]{:S(2)}, u32[]{:S(2)}) collective-permute-start(bf16[512,3072]{1,0:T(8,128)(2,1)S(1)} %copy-done), channel_id=1, source_target_pairs={{0,8},{1,9},{2,10},{3,11},{4,12},{5,13},{6,14},{7,15},{8,0},{9,1},... | collective-permute-start | bytes 9437192 | tf_op jit(solution)/shard_map/ppermute | solution.py:52
  17.3 23.7 %slice-start.3 = ((s8[6291456]{0:T(1024)(128)(4,1)}), s8[2097152]{0:T(1024)(128)(4,1)S(1)}, s32[]{:S(2)}) async-start(s8[6291456]{0:T(1024)(128)(4,1)} %bitcast.4), calls=%async_computation.3 | async-start | bytes 4194304
  17.3 11.1 %collective-permute-start = (bf16[512,1024]{1,0:T(8,128)(2,1)S(1)}, bf16[512,1024]{1,0:T(8,128)(2,1)S(1)}, u32[]{:S(2)}, u32[]{:S(2)}) collective-permute-start(bf16[512,1024]{1,0:T(8,128)(2,1)S(1)} %get-tuple-element.43.refs_0_), channel_id=1, source_target_pairs={{0,8},{1,9},{2,10},{3,11},{4,12},{5,13},{6,14},{7,15},{8,0},{9,1},... | collective-permute-start | bytes 3145736 | tf_op jit(solution)/shard_map/ppermute | solution.py:52
  32.9 16.7 %collective-permute-start.2 = (bf16[4,2,4,64,128]{4,3,2,1,0:T(8,128)(2,1)S(1)}, bf16[4,2,4,64,128]{4,3,2,1,0:T(8,128)(2,1)S(1)}, u32[]{:S(2)}, u32[]{:S(2)}) collective-permute-start(bf16[4,2,4,64,128]{4,3,2,1,0:T(8,128)(2,1)S(1)} %get-tuple-element.46), channel_id=1, source_target_pairs={{0,64},{1,65},{2,66},{3,67},{4,68},{5,69},{6,70},{7,71},{8,10},{9,... | collective-permute-start | bytes 1572872 | tf_op jit(solution)/shard_map/ppermute | solution.py:44
  35.1 11.9 %collective-permute-start.12 = (bf16[4,4,64,128]{3,2,1,0:T(8,128)(2,1)S(1)}, bf16[4,4,64,128]{3,2,1,0:T(8,128)(2,1)S(1)}, u32[]{:S(2)}, u32[]{:S(2)}) collective-permute-start(bf16[4,4,64,128]{3,2,1,0:T(8,128)(2,1)S(1)} %get-tuple-element.59), channel_id=1, source_target_pairs={{0,32},{1,33},{2,34},{3,35},{4,36},{5,37},{6,38},{7,39},{8,40},{9,... | collective-permute-start | bytes 786440 | tf_op jit(solution)/shard_map/ppermute | solution.py:44
  38.9 10.7 %collective-permute-start.3 = (bf16[4,2,4,64,128]{4,3,2,1,0:T(8,128)(2,1)S(1)}, bf16[4,2,4,64,128]{4,3,2,1,0:T(8,128)(2,1)S(1)}, u32[]{:S(2)}, u32[]{:S(2)}) collective-permute-start(bf16[4,2,4,64,128]{4,3,2,1,0:T(8,128)(2,1)S(1)} %get-tuple-element.47), channel_id=1, source_target_pairs={{0,4},{1,5},{2,6},{3,7},{4,64},{5,65},{6,66},{7,67},{8,9},{9,10},{... | collective-permute-start | bytes 1572872 | tf_op jit(solution)/shard_map/ppermute | solution.py:44
  38.9 12.3 %collective-permute-start.4 = (bf16[4,2,4,64,128]{4,3,2,1,0:T(8,128)(2,1)S(1)}, bf16[4,2,4,64,128]{4,3,2,1,0:T(8,128)(2,1)S(1)}, u32[]{:S(2)}, u32[]{:S(2)}) collective-permute-start(bf16[4,2,4,64,128]{4,3,2,1,0:T(8,128)(2,1)S(1)} %get-tuple-element.48), channel_id=1, source_target_pairs={{0,68},{1,69},{2,70},{3,71},{4,0},{5,1},{6,2},{7,3},{8,11},{9,8},{... | collective-permute-start | bytes 1572872 | tf_op jit(solution)/shard_map/ppermute | solution.py:44
  45.4 10.9 %collective-permute-start.6 = (bf16[4,2,4,64,128]{4,3,2,1,0:T(8,128)(2,1)S(1)}, bf16[4,2,4,64,128]{4,3,2,1,0:T(8,128)(2,1)S(1)}, u32[]{:S(2)}, u32[]{:S(2)}) collective-permute-start(bf16[4,2,4,64,128]{4,3,2,1,0:T(8,128)(2,1)S(1)} %get-tuple-element.51), channel_id=1, source_target_pairs={{0,64},{1,65},{2,66},{3,67},{4,68},{5,69},{6,70},{7,71},{8,10},{9,... | collective-permute-start | bytes 1572872 | tf_op jit(solution)/shard_map/ppermute | solution.py:44
  47.0 14.0 %collective-permute-start.7 = (bf16[4,2,4,64,128]{4,3,2,1,0:T(8,128)(2,1)S(1)}, bf16[4,2,4,64,128]{4,3,2,1,0:T(8,128)(2,1)S(1)}, u32[]{:S(2)}, u32[]{:S(2)}) collective-permute-start(bf16[4,2,4,64,128]{4,3,2,1,0:T(8,128)(2,1)S(1)} %get-tuple-element.52), channel_id=1, source_target_pairs={{0,4},{1,5},{2,6},{3,7},{4,64},{5,65},{6,66},{7,67},{8,9},{9,10},{... | collective-permute-start | bytes 1572872 | tf_op jit(solution)/shard_map/ppermute | solution.py:44
  49.6 12.9 %collective-permute-start.8 = (bf16[4,2,4,64,128]{4,3,2,1,0:T(8,128)(2,1)S(1)}, bf16[4,2,4,64,128]{4,3,2,1,0:T(8,128)(2,1)S(1)}, u32[]{:S(2)}, u32[]{:S(2)}) collective-permute-start(bf16[4,2,4,64,128]{4,3,2,1,0:T(8,128)(2,1)S(1)} %get-tuple-element.53), channel_id=1, source_target_pairs={{0,68},{1,69},{2,70},{3,71},{4,0},{5,1},{6,2},{7,3},{8,11},{9,8},{... | collective-permute-start | bytes 1572872 | tf_op jit(solution)/shard_map/ppermute | solution.py:44
  49.6 16.2 %collective-permute-start.13 = (bf16[4,4,64,128]{3,2,1,0:T(8,128)(2,1)S(1)}, bf16[4,4,64,128]{3,2,1,0:T(8,128)(2,1)S(1)}, u32[]{:S(2)}, u32[]{:S(2)}) collective-permute-start(bf16[4,4,64,128]{3,2,1,0:T(8,128)(2,1)S(1)} %get-tuple-element.60), channel_id=1, source_target_pairs={{0,16},{1,17},{2,18},{3,19},{4,20},{5,21},{6,22},{7,23},{8,24},{9,... | collective-permute-start | bytes 786440 | tf_op jit(solution)/shard_map/ppermute | solution.py:44
  51.2 15.9 %collective-permute-start.14 = (bf16[4,4,64,128]{3,2,1,0:T(8,128)(2,1)S(1)}, bf16[4,4,64,128]{3,2,1,0:T(8,128)(2,1)S(1)}, u32[]{:S(2)}, u32[]{:S(2)}) collective-permute-start(bf16[4,4,64,128]{3,2,1,0:T(8,128)(2,1)S(1)} %get-tuple-element.61), channel_id=1, source_target_pairs={{0,48},{1,49},{2,50},{3,51},{4,52},{5,53},{6,54},{7,55},{8,56},{9,... | collective-permute-start | bytes 786440 | tf_op jit(solution)/shard_map/ppermute | solution.py:44
  56.3 13.1 %collective-permute-start.15 = (bf16[4,4,64,128]{3,2,1,0:T(8,128)(2,1)S(1)}, bf16[4,4,64,128]{3,2,1,0:T(8,128)(2,1)S(1)}, u32[]{:S(2)}, u32[]{:S(2)}) collective-permute-start(bf16[4,4,64,128]{3,2,1,0:T(8,128)(2,1)S(1)} %get-tuple-element.63), channel_id=1, source_target_pairs={{0,32},{1,33},{2,34},{3,35},{4,36},{5,37},{6,38},{7,39},{8,40},{9,... | collective-permute-start | bytes 786440 | tf_op jit(solution)/shard_map/ppermute | solution.py:44
  61.0 13.4 %collective-permute-start.16 = (bf16[4,4,64,128]{3,2,1,0:T(8,128)(2,1)S(1)}, bf16[4,4,64,128]{3,2,1,0:T(8,128)(2,1)S(1)}, u32[]{:S(2)}, u32[]{:S(2)}) collective-permute-start(bf16[4,4,64,128]{3,2,1,0:T(8,128)(2,1)S(1)} %get-tuple-element.64), channel_id=1, source_target_pairs={{0,16},{1,17},{2,18},{3,19},{4,20},{5,21},{6,22},{7,23},{8,24},{9,... | collective-permute-start | bytes 786440 | tf_op jit(solution)/shard_map/ppermute | solution.py:44
  62.5 11.8 %collective-permute-start.17 = (bf16[4,4,64,128]{3,2,1,0:T(8,128)(2,1)S(1)}, bf16[4,4,64,128]{3,2,1,0:T(8,128)(2,1)S(1)}, u32[]{:S(2)}, u32[]{:S(2)}) collective-permute-start(bf16[4,4,64,128]{3,2,1,0:T(8,128)(2,1)S(1)} %get-tuple-element.65), channel_id=1, source_target_pairs={{0,48},{1,49},{2,50},{3,51},{4,52},{5,53},{6,54},{7,55},{8,56},{9,... | collective-permute-start | bytes 786440 | tf_op jit(solution)/shard_map/ppermute | solution.py:44
  65.8 14.3 %collective-permute-start.9 = (bf16[2,4,2,64,128]{4,3,2,1,0:T(8,128)(2,1)S(1)}, bf16[2,4,2,64,128]{4,3,2,1,0:T(8,128)(2,1)S(1)}, u32[]{:S(2)}, u32[]{:S(2)}) collective-permute-start(bf16[2,4,2,64,128]{4,3,2,1,0:T(8,128)(2,1)S(1)} %get-tuple-element.55), channel_id=1, source_target_pairs={{0,2},{1,3},{2,0},{3,1},{4,6},{5,7},{6,4},{7,5},{8,40},{9,41},{10,... | collective-permute-start | bytes 786440 | tf_op jit(solution)/shard_map/ppermute | solution.py:44
  67.2 14.7 %collective-permute-start.10 = (bf16[2,4,2,64,128]{4,3,2,1,0:T(8,128)(2,1)S(1)}, bf16[2,4,2,64,128]{4,3,2,1,0:T(8,128)(2,1)S(1)}, u32[]{:S(2)}, u32[]{:S(2)}) collective-permute-start(bf16[2,4,2,64,128]{4,3,2,1,0:T(8,128)(2,1)S(1)} %get-tuple-element.56), channel_id=1, source_target_pairs={{0,1},{1,2},{2,3},{3,0},{4,5},{5,6},{6,7},{7,4},{8,24},{9,25},{10,... | collective-permute-start | bytes 786440 | tf_op jit(solution)/shard_map/ppermute | solution.py:44
  69.3 12.5 %collective-permute-start.11 = (bf16[2,4,2,64,128]{4,3,2,1,0:T(8,128)(2,1)S(1)}, bf16[2,4,2,64,128]{4,3,2,1,0:T(8,128)(2,1)S(1)}, u32[]{:S(2)}, u32[]{:S(2)}) collective-permute-start(bf16[2,4,2,64,128]{4,3,2,1,0:T(8,128)(2,1)S(1)} %get-tuple-element.57), channel_id=1, source_target_pairs={{0,3},{1,0},{2,1},{3,2},{4,7},{5,4},{6,5},{7,6},{8,56},{9,57},{10,... | collective-permute-start | bytes 786440 | tf_op jit(solution)/shard_map/ppermute | solution.py:44
  75.3 11.7 %collective-permute-start.21 = (bf16[2,4,64,128]{3,2,1,0:T(8,128)(2,1)S(1)}, bf16[2,4,64,128]{3,2,1,0:T(8,128)(2,1)S(1)}, u32[]{:S(2)}, u32[]{:S(2)}) collective-permute-start(bf16[2,4,64,128]{3,2,1,0:T(8,128)(2,1)S(1)} %get-tuple-element.71), channel_id=1, source_target_pairs={{0,64},{1,65},{2,66},{3,67},{4,68},{5,69},{6,70},{7,71},{8,72},{9,... | collective-permute-start | bytes 393224 | tf_op jit(solution)/shard_map/ppermute | solution.py:44
  79.8 9.0 %collective-permute-start.22 = (bf16[2,4,64,128]{3,2,1,0:T(8,128)(2,1)S(1)}, bf16[2,4,64,128]{3,2,1,0:T(8,128)(2,1)S(1)}, u32[]{:S(2)}, u32[]{:S(2)}) collective-permute-start(bf16[2,4,64,128]{3,2,1,0:T(8,128)(2,1)S(1)} %get-tuple-element.72), channel_id=1, source_target_pairs={{0,4},{1,5},{2,6},{3,7},{4,64},{5,65},{6,66},{7,67},{8,12},{9,13},... | collective-permute-start | bytes 393224 | tf_op jit(solution)/shard_map/ppermute | solution.py:44
  80.2 8.7 %collective-permute-start.23 = (bf16[2,4,64,128]{3,2,1,0:T(8,128)(2,1)S(1)}, bf16[2,4,64,128]{3,2,1,0:T(8,128)(2,1)S(1)}, u32[]{:S(2)}, u32[]{:S(2)}) collective-permute-start(bf16[2,4,64,128]{3,2,1,0:T(8,128)(2,1)S(1)} %get-tuple-element.73), channel_id=1, source_target_pairs={{0,68},{1,69},{2,70},{3,71},{4,0},{5,1},{6,2},{7,3},{8,76},{9,77},... | collective-permute-start | bytes 393224 | tf_op jit(solution)/shard_map/ppermute | solution.py:44
  82.6 6.9 %collective-permute-start.18 = (bf16[2,2,64,128]{3,2,1,0:T(8,128)(2,1)S(1)}, bf16[2,2,64,128]{3,2,1,0:T(8,128)(2,1)S(1)}, u32[]{:S(2)}, u32[]{:S(2)}) collective-permute-start(bf16[2,2,64,128]{3,2,1,0:T(8,128)(2,1)S(1)} %get-tuple-element.68), channel_id=1, source_target_pairs={{0,32},{1,33},{2,34},{3,35},{4,36},{5,37},{6,38},{7,39},{8,72},{9,... | collective-permute-start | bytes 196616 | tf_op jit(solution)/shard_map/ppermute | solution.py:44
  85.6 5.5 %collective-permute-start.19 = (bf16[2,2,64,128]{3,2,1,0:T(8,128)(2,1)S(1)}, bf16[2,2,64,128]{3,2,1,0:T(8,128)(2,1)S(1)}, u32[]{:S(2)}, u32[]{:S(2)}) collective-permute-start(bf16[2,2,64,128]{3,2,1,0:T(8,128)(2,1)S(1)} %get-tuple-element.69), channel_id=1, source_target_pairs={{0,16},{1,17},{2,18},{3,19},{4,20},{5,21},{6,22},{7,23},{8,12},{9,... | collective-permute-start | bytes 196616 | tf_op jit(solution)/shard_map/ppermute | solution.py:44
  87.0 4.3 %collective-permute-start.20 = (bf16[2,2,64,128]{3,2,1,0:T(8,128)(2,1)S(1)}, bf16[2,2,64,128]{3,2,1,0:T(8,128)(2,1)S(1)}, u32[]{:S(2)}, u32[]{:S(2)}) collective-permute-start(bf16[2,2,64,128]{3,2,1,0:T(8,128)(2,1)S(1)} %get-tuple-element.70), channel_id=1, source_target_pairs={{0,48},{1,49},{2,50},{3,51},{4,52},{5,53},{6,54},{7,55},{8,76},{9,... | collective-permute-start | bytes 196616 | tf_op jit(solution)/shard_map/ppermute | solution.py:44
  91.8 8.7 %collective-permute-start.24 = (f32[2,64,128]{2,1,0:T(8,128)S(1)}, f32[2,64,128]{2,1,0:T(8,128)S(1)}, u32[]{:S(2)}, u32[]{:S(2)}) collective-permute-start(f32[2,64,128]{2,1,0:T(8,128)S(1)} %get-tuple-element.76), channel_id=1, source_target_pairs={{0,8},{1,9},{2,10},{3,11},{4,12},{5,13},{6,14},{7,15},{8,0},{9,1},... | collective-permute-start | bytes 196616 | tf_op jit(solution)/shard_map/ppermute | solution.py:52
  91.9 5.5 %collective-permute-start.25 = (bf16[2,64,128]{2,1,0:T(8,128)(2,1)S(1)}, bf16[2,64,128]{2,1,0:T(8,128)(2,1)S(1)}, u32[]{:S(2)}, u32[]{:S(2)}) collective-permute-start(bf16[2,64,128]{2,1,0:T(8,128)(2,1)S(1)} %get-tuple-element.77), channel_id=1, source_target_pairs={{0,2},{1,3},{2,0},{3,1},{4,6},{5,7},{6,4},{7,5},{8,10},{9,11},{10,... | collective-permute-start | bytes 98312 | tf_op jit(solution)/shard_map/ppermute | solution.py:44
  93.2 4.2 %collective-permute-start.26 = (bf16[2,64,128]{2,1,0:T(8,128)(2,1)S(1)}, bf16[2,64,128]{2,1,0:T(8,128)(2,1)S(1)}, u32[]{:S(2)}, u32[]{:S(2)}) collective-permute-start(bf16[2,64,128]{2,1,0:T(8,128)(2,1)S(1)} %get-tuple-element.78), channel_id=1, source_target_pairs={{0,1},{1,2},{2,3},{3,0},{4,5},{5,6},{6,7},{7,4},{8,9},{9,10},{10,1... | collective-permute-start | bytes 98312 | tf_op jit(solution)/shard_map/ppermute | solution.py:44
  95.4 5.1 %collective-permute-start.27 = (bf16[2,64,128]{2,1,0:T(8,128)(2,1)S(1)}, bf16[2,64,128]{2,1,0:T(8,128)(2,1)S(1)}, u32[]{:S(2)}, u32[]{:S(2)}) collective-permute-start(bf16[2,64,128]{2,1,0:T(8,128)(2,1)S(1)} %get-tuple-element.79), channel_id=1, source_target_pairs={{0,3},{1,0},{2,1},{3,2},{4,7},{5,4},{6,5},{7,6},{8,11},{9,8},{10,9... | collective-permute-start | bytes 98312 | tf_op jit(solution)/shard_map/ppermute | solution.py:44

commit v3 on v2

--- a/solution.py
+++ b/solution.py
@@ -39,7 +39,7 @@
     for index in range(128):
         x, y, z, core = coords(index)
         place = {"x": x, "y": y, "z": z}
-        place[axis0 if core == 0 else axis1] += step
+        place[axis0 if core == 0 else axis1] ^= step
         pairs.append((index, linear(place["x"], place["y"], place["z"], core)))
     return lax.ppermute(value, AXES, pairs)
 
@@ -65,14 +65,14 @@
 ANY = pl.BlockSpec(memory_space=pl.ANY)
 LIM = 12
 CHUNK = 2 * COLORS * LANES
-SPAN = 2 * CHUNK
-SPANS = WIDTH // SPAN
+AHEAD = 5
+SPANS = ((0, 768), (768, 1536), (2304, 1536), (3840, 1536), (5376, 768))
 
 
 def pack_columns(meta, step, block_ref, peer_ref):
     core, own_z = meta[0], meta[3]
     xh, z = step // 4, step % 4
-    j = (z - own_z + 4) % 4
+    j = z ^ own_z
     base = step * CHUNK
     for cp in range(2):
         source = pl.multiple_of(base + cp * 384 + (1 - core) * LANES, LANES)
@@ -83,73 +83,77 @@
     peer_ref[:, pl.ds(target, LANES)] = block_ref[:, pl.ds(source, LANES)]
 
 
-def span(step):
-    return pl.ds(pl.multiple_of(step * SPAN, SPAN), SPAN)
-
-
 def copies(rows_ref, w_ref, w_axis, rows_buf, w_buf, sems):
     def pair(step):
-        w_at = (span(step), slice(None)) if w_axis == 0 else (slice(None), span(step))
+        at = pl.ds(*SPANS[step])
+        w_at = (at, slice(None)) if w_axis == 0 else (slice(None), at)
         return (
-            pltpu.make_async_copy(rows_ref.at[:, span(step)], rows_buf.at[:, span(step)], sems.at[0, step]),
+            pltpu.make_async_copy(rows_ref.at[:, at], rows_buf.at[:, at], sems.at[0, step]),
             pltpu.make_async_copy(w_ref.at[*w_at], w_buf.at[*w_at], sems.at[1, step]),
         )
 
     return pair
 
 
-def preact_kernel(meta, tok_ref, w_ref, out_ref, peer_ref, tok_buf, w_buf, sems):
-    pair = copies(tok_ref, w_ref, 0, tok_buf, w_buf, sems)
-    for step in range(SPANS):
+def stream(pair, work):
+    for step in range(AHEAD):
         for copy in pair(step):
             copy.start()
-    out_ref[...] = jnp.zeros_like(out_ref)
-
-    def body(step, _):
+    for step, (first, width) in enumerate(SPANS):
         for copy in pair(step):
             copy.wait()
-        out_ref[...] += jnp.dot(tok_buf[:, span(step)], w_buf[span(step), :], preferred_element_type=F32)
-        for half in range(2):
-            pack_columns(meta, step * 2 + half, tok_buf, peer_ref)
-        return 0
-
-    lax.fori_loop(0, SPANS, body, 0)
+        if step + AHEAD < len(SPANS):
+            for copy in pair(step + AHEAD):
+                copy.start()
+        work(step, pl.ds(first, width), range(first // CHUNK, (first + width) // CHUNK))
+
+
+def preact_kernel(meta, tok_ref, w_ref, out_ref, peer_ref, tok_buf, w_buf, sems):
+    def work(step, at, groups):
+        part = jnp.dot(tok_buf[:, at], w_buf[at, :], preferred_element_type=F32)
+        if step == 0:
+            out_ref[...] = part
+        else:
+            out_ref[...] += part
+        for group in groups:
+            pack_columns(meta, group, tok_buf, peer_ref)
+
+    stream(copies(tok_ref, w_ref, 0, tok_buf, w_buf, sems), work)
 
 
 def hidden_kernel(
-    meta, grad_ref, w_ref, preact_ref, hid_ref, peer_ref, acc_ref, slope_ref, grad_buf, w_buf, sems
+    meta, grad_ref, w_ref, preact_ref, act_ref, hid_ref, peer_ref, acc_ref, slope_ref, grad_buf, w_buf, sems
 ):
-    pair = copies(grad_ref, w_ref, 1, grad_buf, w_buf, sems)
-    for step in range(SPANS):
-        for copy in pair(step):
-            copy.start()
-    acc_ref[...] = jnp.zeros_like(acc_ref)
-
-    def body(step, _):
-        for copy in pair(step):
-            copy.wait()
-        rows = pl.ds(pl.multiple_of(step * LANES, LANES), LANES)
+    def gelu(block):
+        rows = pl.ds(block * LANES, LANES)
         preact = preact_ref[rows, :].T
         cumul = 0.5 * (1.0 + lax.erf(preact * (1.0 / math.sqrt(2.0))))
         density = jnp.exp(-0.5 * preact * preact) * (1.0 / math.sqrt(2.0 * math.pi))
-        hid_ref[:, rows] = (preact * cumul).astype(BF16)
+        act_ref[:, rows] = (preact * cumul).astype(BF16)
         slope_ref[:, rows] = cumul + preact * density
-        acc_ref[...] += lax.dot_general(
-            w_buf[:, span(step)], grad_buf[:, span(step)], (((1,), (1,)), ((), ())), preferred_element_type=F32
+
+    def work(step, at, groups):
+        if step < TOK // LANES:
+            gelu(step)
+        part = lax.dot_general(
+            w_buf[:, at], grad_buf[:, at], (((1,), (1,)), ((), ())), preferred_element_type=F32
         )
-        for half in range(2):
-            pack_columns(meta, step * 2 + half, grad_buf, peer_ref)
-        return 0
-
-    lax.fori_loop(0, SPANS, body, 0)
-    hid_ref[:, TOK : 2 * TOK] = (acc_ref[...] * slope_ref[...]).astype(BF16)
-
-
-def term_kernel(meta, *refs, which):
+        if step == 0:
+            acc_ref[...] = part
+        elif step + 1 < len(SPANS):
+            acc_ref[...] += part
+        else:
+            hid_ref[...] = ((acc_ref[...] + part) * slope_ref[...]).astype(BF16)
+        for group in groups:
+            pack_columns(meta, group, grad_buf, peer_ref)
+
+    stream(copies(grad_ref, w_ref, 1, grad_buf, w_buf, sems), work)
+
+
+def term_kernel(meta, *refs):
     hid, hid_peer, full, peer = refs[:4]
     major, minor, scr = refs[4:8], refs[8:12], refs[12]
     core, own_x, own_y, own_z = meta[0], meta[1], meta[2], meta[3]
-    lhs = slice((which == 1) * TOK, (which == 1) * TOK + TOK)
 
     def rows(x, y):
         return pl.ds(pl.multiple_of((x % 2) * 256 + y * SUB, SUB), SUB)
@@ -158,16 +162,16 @@
         tiles = []
         for q in range(4):
             if step < 4:
-                group = (q // 2) * 8 + (own_z + step) % 4 * 2 + q % 2
+                group = (q // 2) * 8 + (own_z ^ step) * 2 + q % 2
                 column = group * 384 + core * LANES
             else:
-                group = (q % 2) * 8 + (own_z + (step - 4) * 2 + q // 2) % 4 * 2 + core
+                group = (q % 2) * 8 + (own_z ^ ((step - 4) * 2 + q // 2)) * 2 + core
                 column = group * 384 + 2 * LANES
             tiles.append(full[:, pl.ds(pl.multiple_of(column, LANES), LANES)])
         own = jnp.concatenate(tiles, axis=1)
-        acc = jnp.dot(hid[:, lhs], own, preferred_element_type=F32)
+        acc = jnp.dot(hid[...], own, preferred_element_type=F32)
         other = peer[:, step * 4 * LANES : (step + 1) * 4 * LANES]
-        acc += jnp.dot(hid_peer[:, lhs], other, preferred_element_type=F32)
+        acc += jnp.dot(hid_peer[...], other, preferred_element_type=F32)
         acc = acc.astype(BF16)
         for q in range(4):
             scr[slot, q] = acc[:, q * LANES : (q + 1) * LANES]
@@ -176,16 +180,16 @@
         if step < 4:
             for d in range(4):
                 for w in range(4):
-                    x = (own_x + jnp.where(core == 0, d, w)) % 4
-                    y = (own_y + jnp.where(core == 0, w, d)) % 4
+                    x = own_x ^ jnp.where(core == 0, d, w)
+                    y = own_y ^ jnp.where(core == 0, w, d)
                     for cp in range(2):
                         major[d][step, cp, w] = scr[slot, (x // 2) * 2 + cp, rows(x, y), :]
             return
         for jj in range(2):
             for xo in range(4):
-                x = (own_x + xo) % 4
+                x = own_x ^ xo
                 for yo in range(4):
-                    y = (own_y + yo) % 4
+                    y = own_y ^ yo
                     minor[(step - 4) * 2 + jj][xo, yo] = scr[slot, jj * 2 + x // 2, rows(x, y), :]
 
     matmul(0, 0)
@@ -203,9 +207,9 @@
     return jax.ShapeDtypeStruct(dims, BF16)
 
 
-def term_call(meta, which, hid, hid_peer, full, peer):
+def term_call(meta, hid, hid_peer, full, peer):
     return pl.pallas_call(
-        functools.partial(term_kernel, which=which),
+        term_kernel,
         in_specs=[SMEM] + [VMEM] * 4,
         out_specs=[VMEM] * 8,
         out_shape=[bf16(*MAJOR1)] * 4 + [bf16(*MINOR1)] * 4,
@@ -288,7 +292,11 @@
         in_specs.append(ANY)
         operands.append(after)
     return pl.pallas_call(
-        kernel, in_specs=in_specs, out_specs=[VMEM] * len(shapes), out_shape=shapes, compiler_params=limit(LIM)
+        kernel,
+        in_specs=in_specs,
+        out_specs=[VMEM] * len(shapes),
+        out_shape=shapes,
+        compiler_params=limit(LIM),
     )(*operands)
 
 
@@ -315,7 +323,7 @@
         scratch_shapes=[
             pltpu.VMEM((TOK, WIDTH), BF16),
             pltpu.VMEM((WIDTH, HID), BF16),
-            pltpu.SemaphoreType.DMA((2, SPANS)),
+            pltpu.SemaphoreType.DMA((2, len(SPANS))),
         ],
         compiler_params=limit(50),
         cost_estimate=cost(2 * TOK * HID * WIDTH, 16 * 1024 * 1024),
@@ -323,27 +331,28 @@
     )(meta, tokens, w_up)
     peer_tok = swap(pack_tok)
 
-    hid, pack_grad = pl.pallas_call(
+    act, hid, pack_grad = pl.pallas_call(
         hidden_kernel,
         in_specs=[SMEM, ANY, ANY, VMEM],
-        out_specs=[VMEM] * 2,
-        out_shape=[bf16(HID, 2 * TOK), bf16(TOK, HALF)],
+        out_specs=[VMEM] * 3,
+        out_shape=[bf16(HID, TOK), bf16(HID, TOK), bf16(TOK, HALF)],
         scratch_shapes=[
             pltpu.VMEM((HID, TOK), F32),
             pltpu.VMEM((HID, TOK), F32),
             pltpu.VMEM((TOK, WIDTH), BF16),
             pltpu.VMEM((HID, WIDTH), BF16),
-            pltpu.SemaphoreType.DMA((2, SPANS)),
+            pltpu.SemaphoreType.DMA((2, len(SPANS))),
         ],
         compiler_params=limit(44),
         cost_estimate=cost(2 * TOK * HID * WIDTH, 18 * 1024 * 1024),
         name="hidden",
     )(meta, grad_out, w_down, preact)
     hid_peer = swap(hid)
+    act_peer = swap(act)
     peer_grad = swap(pack_grad)
 
-    up = term_call(meta, 1, hid, hid_peer, tokens, peer_tok)
-    down = term_call(meta, 0, hid, hid_peer, grad_out, peer_grad)
+    up = term_call(meta, hid, hid_peer, tokens, peer_tok)
+    down = term_call(meta, act, act_peer, grad_out, peer_grad)
     up_major, up_minor = ring(up[:4], "x", "y"), ring(up[4:], "z", "z")
     major, minor = ring(down[:4], "x", "y"), ring(down[4:], "z", "z")
 
@@ -355,7 +364,9 @@
     minor = sum_call(minor2_kernel, meta, minor, [bf16(2, SUB, LANES)] * 4, major[0])
     major, last = ring(major, "z", "x"), minor[0]
     minor = ring(minor, "y", "y")
-    keep, send = sum_call(major3_kernel, meta, major, [jax.ShapeDtypeStruct((2, SUB, LANES), F32)] * 2, last)
+    keep, send = sum_call(
+        major3_kernel, meta, major, [jax.ShapeDtypeStruct((2, SUB, LANES), F32)] * 2, last
+    )
     total_tokens = tokens.shape[0] * lax.axis_size("row") * lax.axis_size("col")
     up, down = sum_call(
         functools.partial(final_kernel, factor=1.0 / math.sqrt(total_tokens)),

time: 102 us -> 96.3 us (0.944)
  the two profiles are of different devices: /device:TPU:26 before, /device:TPU:0 now
where the time goes in v3:
time: 96.3 us; the launch traced here: 96.2 us
  starting transfers between devices  42.8 us (44%)
  Pallas kernels  29.5 us (31%)
  waiting for transfers between devices  23 us (24%)
    ppermute x24, starting transfers between devices, shift(): return lax.ppermute(value, AXES, pairs)  41.5 us
    ppermute x24, waiting for transfers between devices, shift(): return lax.ppermute(value, AXES, pairs)  17.5 us
    pallas_call x2, Pallas kernels, term_call(): pl.pallas_call(term_kernel, in_specs=[SMEM] + [VMEM] * 4, out_specs=[VMEM...  8.77 us
    pallas_call x1, Pallas kernels, local(): pl.pallas_call(preact_kernel, in_specs=[SMEM, ANY, ANY], out_specs=[VMEM]...  8.52 us
    pallas_call x1, Pallas kernels, local(): pl.pallas_call(hidden_kernel, in_specs=[SMEM, ANY, ANY, VMEM], out_specs=...  7.05 us
    ppermute x5, waiting for transfers between devices, swap(): return lax.ppermute(value, AXES, pairs)  5.53 us
    pallas_call x6, Pallas kernels, sum_call(): pl.pallas_call(kernel, in_specs=in_specs, out_specs=[VMEM] * len(shapes),...  5.15 us
  transfers between devices with their start and end apart: 29, of which 11 were waited for; matrix products, arithmetic and copies ran while one was open for 0% of the time, Pallas kernels for 20%

profile of v3, /device:TPU:0, one launch (start us, length us, event | category | flops | bytes accessed | tf_op | source)
XLA Modules:
  0.0 96.2 jit_solution(16851108196922691283)
XLA Ops:
  0.7 8.5 %preact.1 = (f32[512,512]{1,0:T(8,128)S(1)}, bf16[512,3072]{1,0:T(8,128)(2,1)}) custom-call(s32[4]{0:T(128)S(1)} %compare_select_fusion.2.meta, bf16[512,6144]{1,0:T(8,128)(2,1)} %refs_2_.3, bf16[6144,512]{1,0:T(8,128)(2,1)} %w_ref.2), custom_call_target="tpu_custom_call" | custom-call | flops 3221225472 | bytes 16777216 | tf_op jit(solution)/shard_map/preact/pallas_call | solution.py:318
  9.4 7.1 %hidden.1 = (bf16[512,512]{1,0:T(8,128)(2,1)S(1)}, bf16[512,512]{1,0:T(8,128)(2,1)S(1)}, bf16[512,3072]{1,0:T(8,128)(2,1)S(1)}) custom-call(s32[4]{0:T(128)S(1)} %compare_select_fusion.2.meta, bf16[512,6144]{1,0:T(8,128)(2,1)} %refs_2_.2, bf16[512,6144]{1,0:T(8,128)(2,1)} %w_ref.3, f32[512,512]{1,0:T(8,128)S(1)} %get-tuple-element.43.preact_ref), custom_call_target="tpu_custom_call" | custom-call | flops 3221225472 | bytes 18874368 | tf_op jit(solution)/shard_map/hidden/pallas_call | solution.py:334
  16.4 0.6 collective-permute-start.1
  17.1 0.1 collective-permute-start.5
  17.1 0.4 collective-permute-start
  17.6 5.5 %collective-permute-done.5.refs_1_ = bf16[512,512]{1,0:T(8,128)(2,1)S(1)} collective-permute-done((bf16[512,512]{1,0:T(8,128)(2,1)S(1)}, bf16[512,512]{1,0:T(8,128)(2,1)S(1)}, u32[]{:S(2)}, u32[]{:S(2)}) %collective-permute-start.5) | collective-permute-done | bytes 524320 | tf_op jit(solution)/shard_map/ppermute | solution.py:52
  23.1 4.4 %shard_map.60 = (bf16[4,2,4,64,128]{4,3,2,1,0:T(8,128)(2,1)S(1)}, bf16[4,2,4,64,128]{4,3,2,1,0:T(8,128)(2,1)S(1)}, bf16[4,2,4,64,128]{4,3,2,1,0:T(8,128)(2,1)S(1...) custom-call(s32[4]{0:T(128)S(1)} %compare_select_fusion.2.meta, ...), custom_call_target="tpu_custom_call" | custom-call | flops 3221225472 | bytes 12582912 | tf_op jit(solution)/shard_map/pallas_call | solution.py:211
  27.5 3.2 %collective-permute-start.7 = (bf16[4,2,4,64,128]{4,3,2,1,0:T(8,128)(2,1)S(1)}, bf16[4,2,4,64,128]{4,3,2,1,0:T(8,128)(2,1)S(1)}, u32[]{:S(2)}, u32[]{:S(2)}) collective-permute-start(bf16[4,2,4,64,128]{4,3,2,1,0:T(8,128)(2,1)S(1)} %get-tuple-element.53), channel_id=1, source_target_pairs={{0,64},{1,65},{2,66},{3,67},{4,68},{5,69},{6,70},{7,71},{8,10},{9,... | collective-permute-start | bytes 1572872 | tf_op jit(solution)/shard_map/ppermute | solution.py:44
  30.7 0.6 collective-permute-start.8
  31.3 0.6 collective-permute-start.9
  31.9 3.9 %collective-permute-start.16 = (bf16[4,4,64,128]{3,2,1,0:T(8,128)(2,1)S(1)}, bf16[4,4,64,128]{3,2,1,0:T(8,128)(2,1)S(1)}, u32[]{:S(2)}, u32[]{:S(2)}) collective-permute-start(bf16[4,4,64,128]{3,2,1,0:T(8,128)(2,1)S(1)} %get-tuple-element.65), channel_id=1, source_target_pairs={{0,32},{1,33},{2,34},{3,35},{4,36},{5,37},{6,38},{7,39},{8,40},{9,... | collective-permute-start | bytes 786440 | tf_op jit(solution)/shard_map/ppermute | solution.py:44
  35.8 4.4 %shard_map.59 = (bf16[4,2,4,64,128]{4,3,2,1,0:T(8,128)(2,1)S(1)}, bf16[4,2,4,64,128]{4,3,2,1,0:T(8,128)(2,1)S(1)}, bf16[4,2,4,64,128]{4,3,2,1,0:T(8,128)(2,1)S(1...) custom-call(s32[4]{0:T(128)S(1)} %compare_select_fusion.2.meta, ...), custom_call_target="tpu_custom_call" | custom-call | flops 3221225472 | bytes 12582912 | tf_op jit(solution)/shard_map/pallas_call | solution.py:211
  40.2 3.0 %collective-permute-start.2 = (bf16[4,2,4,64,128]{4,3,2,1,0:T(8,128)(2,1)S(1)}, bf16[4,2,4,64,128]{4,3,2,1,0:T(8,128)(2,1)S(1)}, u32[]{:S(2)}, u32[]{:S(2)}) collective-permute-start(bf16[4,2,4,64,128]{4,3,2,1,0:T(8,128)(2,1)S(1)} %get-tuple-element.47), channel_id=1, source_target_pairs={{0,64},{1,65},{2,66},{3,67},{4,68},{5,69},{6,70},{7,71},{8,10},{9,... | collective-permute-start | bytes 1572872 | tf_op jit(solution)/shard_map/ppermute | solution.py:44
  43.2 0.6 collective-permute-start.3
  43.8 1.9 %collective-permute-start.4 = (bf16[4,2,4,64,128]{4,3,2,1,0:T(8,128)(2,1)S(1)}, bf16[4,2,4,64,128]{4,3,2,1,0:T(8,128)(2,1)S(1)}, u32[]{:S(2)}, u32[]{:S(2)}) collective-permute-start(bf16[4,2,4,64,128]{4,3,2,1,0:T(8,128)(2,1)S(1)} %get-tuple-element.49), channel_id=1, source_target_pairs={{0,68},{1,69},{2,70},{3,71},{4,64},{5,65},{6,66},{7,67},{8,11},{9,... | collective-permute-start | bytes 1572872 | tf_op jit(solution)/shard_map/ppermute | solution.py:44
  45.8 1.2 %collective-permute-start.17 = (bf16[4,4,64,128]{3,2,1,0:T(8,128)(2,1)S(1)}, bf16[4,4,64,128]{3,2,1,0:T(8,128)(2,1)S(1)}, u32[]{:S(2)}, u32[]{:S(2)}) collective-permute-start(bf16[4,4,64,128]{3,2,1,0:T(8,128)(2,1)S(1)} %get-tuple-element.66), channel_id=1, source_target_pairs={{0,16},{1,17},{2,18},{3,19},{4,20},{5,21},{6,22},{7,23},{8,24},{9,... | collective-permute-start | bytes 786440 | tf_op jit(solution)/shard_map/ppermute | solution.py:44
  47.0 2.6 %collective-permute-start.18 = (bf16[4,4,64,128]{3,2,1,0:T(8,128)(2,1)S(1)}, bf16[4,4,64,128]{3,2,1,0:T(8,128)(2,1)S(1)}, u32[]{:S(2)}, u32[]{:S(2)}) collective-permute-start(bf16[4,4,64,128]{3,2,1,0:T(8,128)(2,1)S(1)} %get-tuple-element.67), channel_id=1, source_target_pairs={{0,48},{1,49},{2,50},{3,51},{4,52},{5,53},{6,54},{7,55},{8,56},{9,... | collective-permute-start | bytes 786440 | tf_op jit(solution)/shard_map/ppermute | solution.py:44
  49.6 1.5 %collective-permute-done.2.refs_1_ = bf16[4,2,4,64,128]{4,3,2,1,0:T(8,128)(2,1)S(1)} collective-permute-done((bf16[4,2,4,64,128]{4,3,2,1,0:T(8,128)(2,1)S(1)}, bf16[4,2,4,64,128]{4,3,2,1,0:T(8,128)(2,1)S(1)}, u32[]{:S(2)}, u32[]{:S(2)}) %collective-permute-start.2) | collective-permute-done | bytes 524320 | tf_op jit(solution)/shard_map/ppermute | solution.py:44
  51.0 2.6 %collective-permute-start.13 = (bf16[4,4,64,128]{3,2,1,0:T(8,128)(2,1)S(1)}, bf16[4,4,64,128]{3,2,1,0:T(8,128)(2,1)S(1)}, u32[]{:S(2)}, u32[]{:S(2)}) collective-permute-start(bf16[4,4,64,128]{3,2,1,0:T(8,128)(2,1)S(1)} %get-tuple-element.61), channel_id=1, source_target_pairs={{0,32},{1,33},{2,34},{3,35},{4,36},{5,37},{6,38},{7,39},{8,40},{9,... | collective-permute-start | bytes 786440 | tf_op jit(solution)/shard_map/ppermute | solution.py:44
  53.6 3.0 %collective-permute-done.3.refs_2_ = bf16[4,2,4,64,128]{4,3,2,1,0:T(8,128)(2,1)S(1)} collective-permute-done((bf16[4,2,4,64,128]{4,3,2,1,0:T(8,128)(2,1)S(1)}, bf16[4,2,4,64,128]{4,3,2,1,0:T(8,128)(2,1)S(1)}, u32[]{:S(2)}, u32[]{:S(2)}) %collective-permute-start.3) | collective-permute-done | bytes 524320 | tf_op jit(solution)/shard_map/ppermute | solution.py:44
  56.6 1.0 %collective-permute-start.14 = (bf16[4,4,64,128]{3,2,1,0:T(8,128)(2,1)S(1)}, bf16[4,4,64,128]{3,2,1,0:T(8,128)(2,1)S(1)}, u32[]{:S(2)}, u32[]{:S(2)}) collective-permute-start(bf16[4,4,64,128]{3,2,1,0:T(8,128)(2,1)S(1)} %get-tuple-element.62), channel_id=1, source_target_pairs={{0,16},{1,17},{2,18},{3,19},{4,20},{5,21},{6,22},{7,23},{8,24},{9,... | collective-permute-start | bytes 786440 | tf_op jit(solution)/shard_map/ppermute | solution.py:44
  57.6 2.2 %collective-permute-start.15 = (bf16[4,4,64,128]{3,2,1,0:T(8,128)(2,1)S(1)}, bf16[4,4,64,128]{3,2,1,0:T(8,128)(2,1)S(1)}, u32[]{:S(2)}, u32[]{:S(2)}) collective-permute-start(bf16[4,4,64,128]{3,2,1,0:T(8,128)(2,1)S(1)} %get-tuple-element.63), channel_id=1, source_target_pairs={{0,48},{1,49},{2,50},{3,51},{4,52},{5,53},{6,54},{7,55},{8,56},{9,... | collective-permute-start | bytes 786440 | tf_op jit(solution)/shard_map/ppermute | solution.py:44
  59.9 1.2 %shard_map.61 = (bf16[2,4,2,64,128]{4,3,2,1,0:T(8,128)(2,1)S(1)}, bf16[2,4,2,64,128]{4,3,2,1,0:T(8,128)(2,1)S(1)}, bf16[2,4,2,64,128]{4,3,2,1,0:T(8,128)(2,1)S(1)}, bf16[2,4,2,64,128]{4,3,2,1,0:T(8,128)(2,1)S(1)}) custom-call(s32[4]{0:T(128)S(1)} %compare_select_fusion.2.meta, bf16[4,2,4,64,128]{4,3,2,1,0:T(8,128)(2,1)S(1)} %get-tuple-element.46.refs_0_, ...), custom_call_target="tpu_custom_call" | custom-call | tf_op jit(solution)/shard_map/pallas_call | solution.py:294
  61.1 3.3 %collective-permute-start.10 = (bf16[2,4,2,64,128]{4,3,2,1,0:T(8,128)(2,1)S(1)}, bf16[2,4,2,64,128]{4,3,2,1,0:T(8,128)(2,1)S(1)}, u32[]{:S(2)}, u32[]{:S(2)}) collective-permute-start(bf16[2,4,2,64,128]{4,3,2,1,0:T(8,128)(2,1)S(1)} %get-tuple-element.57), channel_id=1, source_target_pairs={{0,2},{1,3},{2,0},{3,1},{4,6},{5,7},{6,4},{7,5},{8,40},{9,41},{10,... | collective-permute-start | bytes 786440 | tf_op jit(solution)/shard_map/ppermute | solution.py:44
  64.3 0.7 collective-permute-start.11
  65.0 0.5 collective-permute-start.12
  65.5 1.9 %collective-permute-done.14.refs_2_ = bf16[4,4,64,128]{3,2,1,0:T(8,128)(2,1)S(1)} collective-permute-done((bf16[4,4,64,128]{3,2,1,0:T(8,128)(2,1)S(1)}, bf16[4,4,64,128]{3,2,1,0:T(8,128)(2,1)S(1)}, u32[]{:S(2)}, u32[]{:S(2)}) %collective-permute-start.14) | collective-permute-done | bytes 262176 | tf_op jit(solution)/shard_map/ppermute | solution.py:44
  67.4 3.4 %collective-permute-done.15.refs_3_ = bf16[4,4,64,128]{3,2,1,0:T(8,128)(2,1)S(1)} collective-permute-done((bf16[4,4,64,128]{3,2,1,0:T(8,128)(2,1)S(1)}, bf16[4,4,64,128]{3,2,1,0:T(8,128)(2,1)S(1)}, u32[]{:S(2)}, u32[]{:S(2)}) %collective-permute-start.15) | collective-permute-done | bytes 262176 | tf_op jit(solution)/shard_map/ppermute | solution.py:44
  70.8 0.9 shard_map.62
  71.7 2.1 %collective-permute-start.22 = (bf16[2,4,64,128]{3,2,1,0:T(8,128)(2,1)S(1)}, bf16[2,4,64,128]{3,2,1,0:T(8,128)(2,1)S(1)}, u32[]{:S(2)}, u32[]{:S(2)}) collective-permute-start(bf16[2,4,64,128]{3,2,1,0:T(8,128)(2,1)S(1)} %get-tuple-element.73), channel_id=1, source_target_pairs={{0,64},{1,65},{2,66},{3,67},{4,68},{5,69},{6,70},{7,71},{8,72},{9,... | collective-permute-start | bytes 393224 | tf_op jit(solution)/shard_map/ppermute | solution.py:44
  73.8 2.1 %collective-permute-start.24 = (bf16[2,4,64,128]{3,2,1,0:T(8,128)(2,1)S(1)}, bf16[2,4,64,128]{3,2,1,0:T(8,128)(2,1)S(1)}, u32[]{:S(2)}, u32[]{:S(2)}) collective-permute-start(bf16[2,4,64,128]{3,2,1,0:T(8,128)(2,1)S(1)} %get-tuple-element.75), channel_id=1, source_target_pairs={{0,68},{1,69},{2,70},{3,71},{4,64},{5,65},{6,66},{7,67},{8,76},{9,... | collective-permute-start | bytes 393224 | tf_op jit(solution)/shard_map/ppermute | solution.py:44
  75.9 0.7 shard_map.63
  76.6 2.2 %collective-permute-start.19 = (bf16[2,2,64,128]{3,2,1,0:T(8,128)(2,1)S(1)}, bf16[2,2,64,128]{3,2,1,0:T(8,128)(2,1)S(1)}, u32[]{:S(2)}, u32[]{:S(2)}) collective-permute-start(bf16[2,2,64,128]{3,2,1,0:T(8,128)(2,1)S(1)} %get-tuple-element.70), channel_id=1, source_target_pairs={{0,32},{1,33},{2,34},{3,35},{4,36},{5,37},{6,38},{7,39},{8,72},{9,... | collective-permute-start | bytes 196616 | tf_op jit(solution)/shard_map/ppermute | solution.py:44
  78.7 1.0 %collective-permute-start.20 = (bf16[2,2,64,128]{3,2,1,0:T(8,128)(2,1)S(1)}, bf16[2,2,64,128]{3,2,1,0:T(8,128)(2,1)S(1)}, u32[]{:S(2)}, u32[]{:S(2)}) collective-permute-start(bf16[2,2,64,128]{3,2,1,0:T(8,128)(2,1)S(1)} %get-tuple-element.71), channel_id=1, source_target_pairs={{0,16},{1,17},{2,18},{3,19},{4,20},{5,21},{6,22},{7,23},{8,12},{9,... | collective-permute-start | bytes 196616 | tf_op jit(solution)/shard_map/ppermute | solution.py:44
  79.8 1.9 %collective-permute-start.21 = (bf16[2,2,64,128]{3,2,1,0:T(8,128)(2,1)S(1)}, bf16[2,2,64,128]{3,2,1,0:T(8,128)(2,1)S(1)}, u32[]{:S(2)}, u32[]{:S(2)}) collective-permute-start(bf16[2,2,64,128]{3,2,1,0:T(8,128)(2,1)S(1)} %get-tuple-element.72), channel_id=1, source_target_pairs={{0,48},{1,49},{2,50},{3,51},{4,52},{5,53},{6,54},{7,55},{8,76},{9,... | collective-permute-start | bytes 196616 | tf_op jit(solution)/shard_map/ppermute | solution.py:44
  81.7 0.6 shard_map.64
  82.3 0.1 collective-permute-done.19.refs_1_
  82.4 0.6 collective-permute-done.20.refs_2_
  83.0 2.2 %collective-permute-done.21.refs_3_ = bf16[2,2,64,128]{3,2,1,0:T(8,128)(2,1)S(1)} collective-permute-done((bf16[2,2,64,128]{3,2,1,0:T(8,128)(2,1)S(1)}, bf16[2,2,64,128]{3,2,1,0:T(8,128)(2,1)S(1)}, u32[]{:S(2)}, u32[]{:S(2)}) %collective-permute-start.21) | collective-permute-done | bytes 65568 | tf_op jit(solution)/shard_map/ppermute | solution.py:44
  85.2 0.6 shard_map.65
  85.8 0.1 collective-permute-start.25
  85.9 3.3 %collective-permute-start.26 = (bf16[2,64,128]{2,1,0:T(8,128)(2,1)S(1)}, bf16[2,64,128]{2,1,0:T(8,128)(2,1)S(1)}, u32[]{:S(2)}, u32[]{:S(2)}) collective-permute-start(bf16[2,64,128]{2,1,0:T(8,128)(2,1)S(1)} %get-tuple-element.79), channel_id=1, source_target_pairs={{0,2},{1,3},{2,0},{3,1},{4,6},{5,7},{6,4},{7,5},{8,10},{9,11},{10,... | collective-permute-start | bytes 98312 | tf_op jit(solution)/shard_map/ppermute | solution.py:44
  89.2 0.7 collective-permute-start.27
  89.9 0.4 collective-permute-start.28
  90.3 1.2 %collective-permute-done.26.p1 = bf16[2,64,128]{2,1,0:T(8,128)(2,1)S(1)} collective-permute-done((bf16[2,64,128]{2,1,0:T(8,128)(2,1)S(1)}, bf16[2,64,128]{2,1,0:T(8,128)(2,1)S(1)}, u32[]{:S(2)}, u32[]{:S(2)}) %collective-permute-start.26) | collective-permute-done | bytes 32800 | tf_op jit(solution)/shard_map/ppermute | solution.py:44
  91.4 1.7 %collective-permute-done.27.p2 = bf16[2,64,128]{2,1,0:T(8,128)(2,1)S(1)} collective-permute-done((bf16[2,64,128]{2,1,0:T(8,128)(2,1)S(1)}, bf16[2,64,128]{2,1,0:T(8,128)(2,1)S(1)}, u32[]{:S(2)}, u32[]{:S(2)}) %collective-permute-start.27) | collective-permute-done | bytes 32800 | tf_op jit(solution)/shard_map/ppermute | solution.py:44
  93.1 1.9 %collective-permute-done.28.p3 = bf16[2,64,128]{2,1,0:T(8,128)(2,1)S(1)} collective-permute-done((bf16[2,64,128]{2,1,0:T(8,128)(2,1)S(1)}, bf16[2,64,128]{2,1,0:T(8,128)(2,1)S(1)}, u32[]{:S(2)}, u32[]{:S(2)}) %collective-permute-start.28) | collective-permute-done | bytes 32800 | tf_op jit(solution)/shard_map/ppermute | solution.py:44
  95.0 1.2 %shard_map.66 = (f32[64,384]{1,0:T(8,128)}, f32[64,384]{1,0:T(8,128)}) custom-call(s32[4]{0:T(128)S(1)} %compare_select_fusion.2.meta, f32[2,64,128]{2,1,0:T(8,128)S(1)} %get-tuple-element.77.keep, f32[2,64,128]{2,1,0:T(8,128)S(1)} %collective-permute-done.25.got, bf16[2,64,128]{2,1,0:T(8,128)(2,1)S(1)} %get-tuple-element.76.refs_4_.p0, ...), custom_call_target="tpu_custom_call" | custom-call | tf_op jit(solution)/shard_map/pallas_call | solution.py:294
  (31 shorter events, 0.2 us)
Async XLA Ops:
  0.7 22.4 %slice-start = ((s8[6291456]{0:T(1024)(128)(4,1)}), s8[2097152]{0:T(1024)(128)(4,1)S(1)}, s32[]{:S(2)}) async-start(s8[6291456]{0:T(1024)(128)(4,1)} %bitcast.2), calls=%async_computation | async-start | bytes 4194304
  9.3 13.8 %collective-permute-start.6 = (bf16[512,3072]{1,0:T(8,128)(2,1)}, bf16[512,3072]{1,0:T(8,128)(2,1)S(1)}, u32[]{:S(2)}, u32[]{:S(2)}) collective-permute-start(bf16[512,3072]{1,0:T(8,128)(2,1)} %get-tuple-element.51), channel_id=1, source_target_pairs={{0,8},{1,9},{2,10},{3,11},{4,12},{5,13},{6,14},{7,15},{8,0},{9,1},... | collective-permute-start | bytes 9437192 | tf_op jit(solution)/shard_map/ppermute | solution.py:52
  9.4 13.7 %slice-start.1 = ((s8[6291456]{0:T(1024)(128)(4,1)}), s8[4194304]{0:T(1024)(128)(4,1)S(1)}, s32[]{:S(2)}) async-start(s8[6291456]{0:T(1024)(128)(4,1)} %bitcast.2), calls=%async_computation.1 | async-start | bytes 8388608
  16.4 19.3 %slice-start.2 = ((s8[6291456]{0:T(1024)(128)(4,1)}), s8[4194304]{0:T(1024)(128)(4,1)S(1)}, s32[]{:S(2)}) async-start(s8[6291456]{0:T(1024)(128)(4,1)} %bitcast.4), calls=%async_computation.2 | async-start | bytes 8388608
  16.4 19.3 %collective-permute-start.1 = (bf16[512,3072]{1,0:T(8,128)(2,1)S(1)}, bf16[512,3072]{1,0:T(8,128)(2,1)S(1)}, u32[]{:S(2)}, u32[]{:S(2)}) collective-permute-start(bf16[512,3072]{1,0:T(8,128)(2,1)S(1)} %get-tuple-element.45), channel_id=1, source_target_pairs={{0,8},{1,9},{2,10},{3,11},{4,12},{5,13},{6,14},{7,15},{8,0},{9,1},... | collective-permute-start | bytes 9437192 | tf_op jit(solution)/shard_map/ppermute | solution.py:52
  17.1 6.0 %collective-permute-start.5 = (bf16[512,512]{1,0:T(8,128)(2,1)S(1)}, bf16[512,512]{1,0:T(8,128)(2,1)S(1)}, u32[]{:S(2)}, u32[]{:S(2)}) collective-permute-start(bf16[512,512]{1,0:T(8,128)(2,1)S(1)} %get-tuple-element.50.refs_0_), channel_id=1, source_target_pairs={{0,8},{1,9},{2,10},{3,11},{4,12},{5,13},{6,14},{7,15},{8,0},{9,1},... | collective-permute-start | bytes 1572872 | tf_op jit(solution)/shard_map/ppermute | solution.py:52
  17.1 18.6 %slice-start.3 = ((s8[6291456]{0:T(1024)(128)(4,1)}), s8[2097152]{0:T(1024)(128)(4,1)S(1)}, s32[]{:S(2)}) async-start(s8[6291456]{0:T(1024)(128)(4,1)} %bitcast.4), calls=%async_computation.3 | async-start | bytes 4194304
  17.1 14.7 %collective-permute-start = (bf16[512,512]{1,0:T(8,128)(2,1)S(1)}, bf16[512,512]{1,0:T(8,128)(2,1)S(1)}, u32[]{:S(2)}, u32[]{:S(2)}) collective-permute-start(bf16[512,512]{1,0:T(8,128)(2,1)S(1)} %get-tuple-element.44.refs_0_), channel_id=1, source_target_pairs={{0,8},{1,9},{2,10},{3,11},{4,12},{5,13},{6,14},{7,15},{8,0},{9,1},... | collective-permute-start | bytes 1572872 | tf_op jit(solution)/shard_map/ppermute | solution.py:52
  27.5 16.3 %collective-permute-start.7 = (bf16[4,2,4,64,128]{4,3,2,1,0:T(8,128)(2,1)S(1)}, bf16[4,2,4,64,128]{4,3,2,1,0:T(8,128)(2,1)S(1)}, u32[]{:S(2)}, u32[]{:S(2)}) collective-permute-start(bf16[4,2,4,64,128]{4,3,2,1,0:T(8,128)(2,1)S(1)} %get-tuple-element.53), channel_id=1, source_target_pairs={{0,64},{1,65},{2,66},{3,67},{4,68},{5,69},{6,70},{7,71},{8,10},{9,... | collective-permute-start | bytes 1572872 | tf_op jit(solution)/shard_map/ppermute | solution.py:44
  30.7 15.0 %collective-permute-start.8 = (bf16[4,2,4,64,128]{4,3,2,1,0:T(8,128)(2,1)S(1)}, bf16[4,2,4,64,128]{4,3,2,1,0:T(8,128)(2,1)S(1)}, u32[]{:S(2)}, u32[]{:S(2)}) collective-permute-start(bf16[4,2,4,64,128]{4,3,2,1,0:T(8,128)(2,1)S(1)} %get-tuple-element.54), channel_id=1, source_target_pairs={{0,4},{1,5},{2,6},{3,7},{4,0},{5,1},{6,2},{7,3},{8,9},{9,8},{10,11... | collective-permute-start | bytes 1572872 | tf_op jit(solution)/shard_map/ppermute | solution.py:44
  31.3 15.7 %collective-permute-start.9 = (bf16[4,2,4,64,128]{4,3,2,1,0:T(8,128)(2,1)S(1)}, bf16[4,2,4,64,128]{4,3,2,1,0:T(8,128)(2,1)S(1)}, u32[]{:S(2)}, u32[]{:S(2)}) collective-permute-start(bf16[4,2,4,64,128]{4,3,2,1,0:T(8,128)(2,1)S(1)} %get-tuple-element.55), channel_id=1, source_target_pairs={{0,68},{1,69},{2,70},{3,71},{4,64},{5,65},{6,66},{7,67},{8,11},{9,... | collective-permute-start | bytes 1572872 | tf_op jit(solution)/shard_map/ppermute | solution.py:44
  31.9 11.3 %collective-permute-start.16 = (bf16[4,4,64,128]{3,2,1,0:T(8,128)(2,1)S(1)}, bf16[4,4,64,128]{3,2,1,0:T(8,128)(2,1)S(1)}, u32[]{:S(2)}, u32[]{:S(2)}) collective-permute-start(bf16[4,4,64,128]{3,2,1,0:T(8,128)(2,1)S(1)} %get-tuple-element.65), channel_id=1, source_target_pairs={{0,32},{1,33},{2,34},{3,35},{4,36},{5,37},{6,38},{7,39},{8,40},{9,... | collective-permute-start | bytes 786440 | tf_op jit(solution)/shard_map/ppermute | solution.py:44
  40.2 10.9 %collective-permute-start.2 = (bf16[4,2,4,64,128]{4,3,2,1,0:T(8,128)(2,1)S(1)}, bf16[4,2,4,64,128]{4,3,2,1,0:T(8,128)(2,1)S(1)}, u32[]{:S(2)}, u32[]{:S(2)}) collective-permute-start(bf16[4,2,4,64,128]{4,3,2,1,0:T(8,128)(2,1)S(1)} %get-tuple-element.47), channel_id=1, source_target_pairs={{0,64},{1,65},{2,66},{3,67},{4,68},{5,69},{6,70},{7,71},{8,10},{9,... | collective-permute-start | bytes 1572872 | tf_op jit(solution)/shard_map/ppermute | solution.py:44
  43.2 13.4 %collective-permute-start.3 = (bf16[4,2,4,64,128]{4,3,2,1,0:T(8,128)(2,1)S(1)}, bf16[4,2,4,64,128]{4,3,2,1,0:T(8,128)(2,1)S(1)}, u32[]{:S(2)}, u32[]{:S(2)}) collective-permute-start(bf16[4,2,4,64,128]{4,3,2,1,0:T(8,128)(2,1)S(1)} %get-tuple-element.48), channel_id=1, source_target_pairs={{0,4},{1,5},{2,6},{3,7},{4,0},{5,1},{6,2},{7,3},{8,9},{9,8},{10,11... | collective-permute-start | bytes 1572872 | tf_op jit(solution)/shard_map/ppermute | solution.py:44
  43.8 13.8 %collective-permute-start.4 = (bf16[4,2,4,64,128]{4,3,2,1,0:T(8,128)(2,1)S(1)}, bf16[4,2,4,64,128]{4,3,2,1,0:T(8,128)(2,1)S(1)}, u32[]{:S(2)}, u32[]{:S(2)}) collective-permute-start(bf16[4,2,4,64,128]{4,3,2,1,0:T(8,128)(2,1)S(1)} %get-tuple-element.49), channel_id=1, source_target_pairs={{0,68},{1,69},{2,70},{3,71},{4,64},{5,65},{6,66},{7,67},{8,11},{9,... | collective-permute-start | bytes 1572872 | tf_op jit(solution)/shard_map/ppermute | solution.py:44
  45.8 15.3 %collective-permute-start.17 = (bf16[4,4,64,128]{3,2,1,0:T(8,128)(2,1)S(1)}, bf16[4,4,64,128]{3,2,1,0:T(8,128)(2,1)S(1)}, u32[]{:S(2)}, u32[]{:S(2)}) collective-permute-start(bf16[4,4,64,128]{3,2,1,0:T(8,128)(2,1)S(1)} %get-tuple-element.66), channel_id=1, source_target_pairs={{0,16},{1,17},{2,18},{3,19},{4,20},{5,21},{6,22},{7,23},{8,24},{9,... | collective-permute-start | bytes 786440 | tf_op jit(solution)/shard_map/ppermute | solution.py:44
  47.0 17.4 %collective-permute-start.18 = (bf16[4,4,64,128]{3,2,1,0:T(8,128)(2,1)S(1)}, bf16[4,4,64,128]{3,2,1,0:T(8,128)(2,1)S(1)}, u32[]{:S(2)}, u32[]{:S(2)}) collective-permute-start(bf16[4,4,64,128]{3,2,1,0:T(8,128)(2,1)S(1)} %get-tuple-element.67), channel_id=1, source_target_pairs={{0,48},{1,49},{2,50},{3,51},{4,52},{5,53},{6,54},{7,55},{8,56},{9,... | collective-permute-start | bytes 786440 | tf_op jit(solution)/shard_map/ppermute | solution.py:44
  51.0 14.0 %collective-permute-start.13 = (bf16[4,4,64,128]{3,2,1,0:T(8,128)(2,1)S(1)}, bf16[4,4,64,128]{3,2,1,0:T(8,128)(2,1)S(1)}, u32[]{:S(2)}, u32[]{:S(2)}) collective-permute-start(bf16[4,4,64,128]{3,2,1,0:T(8,128)(2,1)S(1)} %get-tuple-element.61), channel_id=1, source_target_pairs={{0,32},{1,33},{2,34},{3,35},{4,36},{5,37},{6,38},{7,39},{8,40},{9,... | collective-permute-start | bytes 786440 | tf_op jit(solution)/shard_map/ppermute | solution.py:44
  56.6 10.8 %collective-permute-start.14 = (bf16[4,4,64,128]{3,2,1,0:T(8,128)(2,1)S(1)}, bf16[4,4,64,128]{3,2,1,0:T(8,128)(2,1)S(1)}, u32[]{:S(2)}, u32[]{:S(2)}) collective-permute-start(bf16[4,4,64,128]{3,2,1,0:T(8,128)(2,1)S(1)} %get-tuple-element.62), channel_id=1, source_target_pairs={{0,16},{1,17},{2,18},{3,19},{4,20},{5,21},{6,22},{7,23},{8,24},{9,... | collective-permute-start | bytes 786440 | tf_op jit(solution)/shard_map/ppermute | solution.py:44
  57.6 13.2 %collective-permute-start.15 = (bf16[4,4,64,128]{3,2,1,0:T(8,128)(2,1)S(1)}, bf16[4,4,64,128]{3,2,1,0:T(8,128)(2,1)S(1)}, u32[]{:S(2)}, u32[]{:S(2)}) collective-permute-start(bf16[4,4,64,128]{3,2,1,0:T(8,128)(2,1)S(1)} %get-tuple-element.63), channel_id=1, source_target_pairs={{0,48},{1,49},{2,50},{3,51},{4,52},{5,53},{6,54},{7,55},{8,56},{9,... | collective-permute-start | bytes 786440 | tf_op jit(solution)/shard_map/ppermute | solution.py:44
  61.1 12.7 %collective-permute-start.10 = (bf16[2,4,2,64,128]{4,3,2,1,0:T(8,128)(2,1)S(1)}, bf16[2,4,2,64,128]{4,3,2,1,0:T(8,128)(2,1)S(1)}, u32[]{:S(2)}, u32[]{:S(2)}) collective-permute-start(bf16[2,4,2,64,128]{4,3,2,1,0:T(8,128)(2,1)S(1)} %get-tuple-element.57), channel_id=1, source_target_pairs={{0,2},{1,3},{2,0},{3,1},{4,6},{5,7},{6,4},{7,5},{8,40},{9,41},{10,... | collective-permute-start | bytes 786440 | tf_op jit(solution)/shard_map/ppermute | solution.py:44
  64.3 11.6 %collective-permute-start.11 = (bf16[2,4,2,64,128]{4,3,2,1,0:T(8,128)(2,1)S(1)}, bf16[2,4,2,64,128]{4,3,2,1,0:T(8,128)(2,1)S(1)}, u32[]{:S(2)}, u32[]{:S(2)}) collective-permute-start(bf16[2,4,2,64,128]{4,3,2,1,0:T(8,128)(2,1)S(1)} %get-tuple-element.58), channel_id=1, source_target_pairs={{0,1},{1,0},{2,3},{3,2},{4,5},{5,4},{6,7},{7,6},{8,24},{9,25},{10,... | collective-permute-start | bytes 786440 | tf_op jit(solution)/shard_map/ppermute | solution.py:44
  65.0 10.9 %collective-permute-start.12 = (bf16[2,4,2,64,128]{4,3,2,1,0:T(8,128)(2,1)S(1)}, bf16[2,4,2,64,128]{4,3,2,1,0:T(8,128)(2,1)S(1)}, u32[]{:S(2)}, u32[]{:S(2)}) collective-permute-start(bf16[2,4,2,64,128]{4,3,2,1,0:T(8,128)(2,1)S(1)} %get-tuple-element.59), channel_id=1, source_target_pairs={{0,3},{1,2},{2,1},{3,0},{4,7},{5,6},{6,5},{7,4},{8,56},{9,57},{10,... | collective-permute-start | bytes 786440 | tf_op jit(solution)/shard_map/ppermute | solution.py:44
  71.7 8.1 %collective-permute-start.22 = (bf16[2,4,64,128]{3,2,1,0:T(8,128)(2,1)S(1)}, bf16[2,4,64,128]{3,2,1,0:T(8,128)(2,1)S(1)}, u32[]{:S(2)}, u32[]{:S(2)}) collective-permute-start(bf16[2,4,64,128]{3,2,1,0:T(8,128)(2,1)S(1)} %get-tuple-element.73), channel_id=1, source_target_pairs={{0,64},{1,65},{2,66},{3,67},{4,68},{5,69},{6,70},{7,71},{8,72},{9,... | collective-permute-start | bytes 393224 | tf_op jit(solution)/shard_map/ppermute | solution.py:44
  73.8 7.9 %collective-permute-start.23 = (bf16[2,4,64,128]{3,2,1,0:T(8,128)(2,1)S(1)}, bf16[2,4,64,128]{3,2,1,0:T(8,128)(2,1)S(1)}, u32[]{:S(2)}, u32[]{:S(2)}) collective-permute-start(bf16[2,4,64,128]{3,2,1,0:T(8,128)(2,1)S(1)} %get-tuple-element.74), channel_id=1, source_target_pairs={{0,4},{1,5},{2,6},{3,7},{4,0},{5,1},{6,2},{7,3},{8,12},{9,13},{10,... | collective-permute-start | bytes 393224 | tf_op jit(solution)/shard_map/ppermute | solution.py:44
  73.8 7.9 %collective-permute-start.24 = (bf16[2,4,64,128]{3,2,1,0:T(8,128)(2,1)S(1)}, bf16[2,4,64,128]{3,2,1,0:T(8,128)(2,1)S(1)}, u32[]{:S(2)}, u32[]{:S(2)}) collective-permute-start(bf16[2,4,64,128]{3,2,1,0:T(8,128)(2,1)S(1)} %get-tuple-element.75), channel_id=1, source_target_pairs={{0,68},{1,69},{2,70},{3,71},{4,64},{5,65},{6,66},{7,67},{8,76},{9,... | collective-permute-start | bytes 393224 | tf_op jit(solution)/shard_map/ppermute | solution.py:44
  76.6 5.8 %collective-permute-start.19 = (bf16[2,2,64,128]{3,2,1,0:T(8,128)(2,1)S(1)}, bf16[2,2,64,128]{3,2,1,0:T(8,128)(2,1)S(1)}, u32[]{:S(2)}, u32[]{:S(2)}) collective-permute-start(bf16[2,2,64,128]{3,2,1,0:T(8,128)(2,1)S(1)} %get-tuple-element.70), channel_id=1, source_target_pairs={{0,32},{1,33},{2,34},{3,35},{4,36},{5,37},{6,38},{7,39},{8,72},{9,... | collective-permute-start | bytes 196616 | tf_op jit(solution)/shard_map/ppermute | solution.py:44
  78.7 4.3 %collective-permute-start.20 = (bf16[2,2,64,128]{3,2,1,0:T(8,128)(2,1)S(1)}, bf16[2,2,64,128]{3,2,1,0:T(8,128)(2,1)S(1)}, u32[]{:S(2)}, u32[]{:S(2)}) collective-permute-start(bf16[2,2,64,128]{3,2,1,0:T(8,128)(2,1)S(1)} %get-tuple-element.71), channel_id=1, source_target_pairs={{0,16},{1,17},{2,18},{3,19},{4,20},{5,21},{6,22},{7,23},{8,12},{9,... | collective-permute-start | bytes 196616 | tf_op jit(solution)/shard_map/ppermute | solution.py:44
  79.8 5.5 %collective-permute-start.21 = (bf16[2,2,64,128]{3,2,1,0:T(8,128)(2,1)S(1)}, bf16[2,2,64,128]{3,2,1,0:T(8,128)(2,1)S(1)}, u32[]{:S(2)}, u32[]{:S(2)}) collective-permute-start(bf16[2,2,64,128]{3,2,1,0:T(8,128)(2,1)S(1)} %get-tuple-element.72), channel_id=1, source_target_pairs={{0,48},{1,49},{2,50},{3,51},{4,52},{5,53},{6,54},{7,55},{8,76},{9,... | collective-permute-start | bytes 196616 | tf_op jit(solution)/shard_map/ppermute | solution.py:44
  85.8 9.2 %collective-permute-start.25 = (f32[2,64,128]{2,1,0:T(8,128)S(1)}, f32[2,64,128]{2,1,0:T(8,128)S(1)}, u32[]{:S(2)}, u32[]{:S(2)}) collective-permute-start(f32[2,64,128]{2,1,0:T(8,128)S(1)} %get-tuple-element.78), channel_id=1, source_target_pairs={{0,8},{1,9},{2,10},{3,11},{4,12},{5,13},{6,14},{7,15},{8,0},{9,1},... | collective-permute-start | bytes 196616 | tf_op jit(solution)/shard_map/ppermute | solution.py:52
  85.9 5.5 %collective-permute-start.26 = (bf16[2,64,128]{2,1,0:T(8,128)(2,1)S(1)}, bf16[2,64,128]{2,1,0:T(8,128)(2,1)S(1)}, u32[]{:S(2)}, u32[]{:S(2)}) collective-permute-start(bf16[2,64,128]{2,1,0:T(8,128)(2,1)S(1)} %get-tuple-element.79), channel_id=1, source_target_pairs={{0,2},{1,3},{2,0},{3,1},{4,6},{5,7},{6,4},{7,5},{8,10},{9,11},{10,... | collective-permute-start | bytes 98312 | tf_op jit(solution)/shard_map/ppermute | solution.py:44
  89.2 3.9 %collective-permute-start.27 = (bf16[2,64,128]{2,1,0:T(8,128)(2,1)S(1)}, bf16[2,64,128]{2,1,0:T(8,128)(2,1)S(1)}, u32[]{:S(2)}, u32[]{:S(2)}) collective-permute-start(bf16[2,64,128]{2,1,0:T(8,128)(2,1)S(1)} %get-tuple-element.80), channel_id=1, source_target_pairs={{0,1},{1,0},{2,3},{3,2},{4,5},{5,4},{6,7},{7,6},{8,9},{9,8},{10,11... | collective-permute-start | bytes 98312 | tf_op jit(solution)/shard_map/ppermute | solution.py:44
  89.9 5.1 %collective-permute-start.28 = (bf16[2,64,128]{2,1,0:T(8,128)(2,1)S(1)}, bf16[2,64,128]{2,1,0:T(8,128)(2,1)S(1)}, u32[]{:S(2)}, u32[]{:S(2)}) collective-permute-start(bf16[2,64,128]{2,1,0:T(8,128)(2,1)S(1)} %get-tuple-element.81), channel_id=1, source_target_pairs={{0,3},{1,2},{2,1},{3,0},{4,7},{5,6},{6,5},{7,4},{8,11},{9,10},{10,... | collective-permute-start | bytes 98312 | tf_op jit(solution)/shard_map/ppermute | solution.py:44
